TPU v7x, 512 devices: a whole 4x8x8 slice. The times are simulated.
512 devices in a mesh: gy: 64 (over z, y_lo, core), gz: 8 (over y_hi, x).
Axes of the slice: x: 4, y: 8 (y_hi: 2, y_lo: 4; y = y_hi * 4 + y_lo), z: 8, core: 2. Of those that a mesh axis runs over, the one named last changes fastest.
Arguments:
- omega: float32 [3, 1024, 512, 128], P(None, 'gy', 'gz'), may hold values from -6 to 6
- velocity: float32 [3, 1024, 512, 128], P(None, 'gy', 'gz'), may hold values from -6 to 6
- point_owner: int32 [1152], replicated, may hold values from 2 to 477, as said below
- point_cells: int32 [3, 1152], replicated, may hold values from 1 to 125, as said below
- point_frac: float32 [3, 1152], replicated, may hold values from 0 to 1
- chord: float32 [1152], replicated, may hold values from 0.2 to 1
- twist: float32 [1152], replicated, may hold values from -0.3 to 0.3
- angle_step: int32 [1], replicated, may hold values from 0 to 719
Outputs:
- omega_out: float32 [3, 1024, 512, 128], P(None, 'gy', 'gz')
- blade_sources: float32 [3, 1152], replicated
Inputs may be any that keep to these rules, and one draw needn't show every extreme that they name: `point_owner`: turbine t's points lie in spanwise blocks t * 10 to (t + 1) * 10 - 1 and in the 4 vertical blocks from (4) // 2 on; no block holds more than 9 points, and in every turbine one block holds exactly 9. `point_cells`: streamwise cells lie in 1 to 125, spanwise in 1 to 13, vertical in 1 to 61; all points of a turbine share one streamwise cell.
All inputs are finite; a program needn't handle non-finite values.
Results may differ from a plain program's by a relative error of at most 0.0003.
Values sent between devices are 32-bit elements; how exact they have to be, the bound alone decides.
A program may use at most 128 MiB of HBM per device.

v0:
```python
import jax
import jax.numpy as jnp
from jax import lax
from jax.sharding import Mesh
from jax.sharding import PartitionSpec as P

TURBINES = 6
BLADES = 3
BP = 64
GY = ("gy_0", "gy_1", "gy_2")
GZ = ("gz_0", "gz_1")
GY_GZ = ("gy_0", "gy_1", "gy_2", "gz_0", "gz_1")


section_step = 0.4
viscosity = 0.05
tip_speed = 3.0
turn_step = 2.0 * 3.141592653589793 / 720.0


def by_axis(x, axes):
    for axis in axes:
        x = lax.psum(x, axis)
    return x


def with_halo(x, sides, width):
    edges = {}
    for axis, dim in sides:
        size, length = (lax.axis_size(axis), x.shape[dim])
        up = [(i, (i + 1) % size) for i in range(size - 1)]
        last = lax.slice_in_dim(x, length - width, length, axis=dim)
        initial = lax.slice_in_dim(x, 0, width, axis=dim)
        edges[dim] = (
            lax.ppermute(last, axis, up),
            lax.ppermute(initial, axis, [(b, a) for a, b in up]),
        )
    done = []
    for _, dim in sides:
        low, high = edges[dim]
        around = [(width, width) if d in done else (0, 0) for d in range(x.ndim)]
        x = jnp.concatenate([jnp.pad(low, around), x, jnp.pad(high, around)], axis=dim)
        done.append(dim)
    return x


def with_halo_2(x, sides, width):
    for axis, dim in sides:
        size, length = (lax.axis_size(axis), x.shape[dim])
        up = [(i, (i + 1) % size) for i in range(size - 1)]
        down = [(j, i) for i, j in up]
        last = lax.slice_in_dim(x, length - width, length, axis=dim)
        initial = lax.slice_in_dim(x, 0, width, axis=dim)
        before = lax.ppermute(last, axis, up)
        after = lax.ppermute(initial, axis, down)
        x = jnp.concatenate([before, x, after], axis=dim)
    return x


def remesh_kernel(shift):
    mag = jnp.abs(shift)
    inner = 1.0 - 2.5 * mag * mag + 1.5 * mag * mag * mag
    outer = 0.5 * (2.0 - mag) * (2.0 - mag) * (1.0 - mag)
    return jnp.where(mag < 1.0, inner, jnp.where(mag < 2.0, outer, 0.0))


def shifted(padded, axis, offset):
    index = []
    for dim in range(4):
        if dim == 0:
            index.append(slice(None))
        elif dim == axis:
            index.append(slice(offset, offset + padded.shape[dim] - 4))
        else:
            index.append(slice(2, padded.shape[dim] - 2))
    return padded[tuple(index)]


def centered_first(padded, axis):
    return (
        shifted(padded, axis, 0)
        - 8.0 * shifted(padded, axis, 1)
        + 8.0 * shifted(padded, axis, 3)
        - shifted(padded, axis, 4)
    ) / 12.0


def centered_second(padded, axis):
    return (
        -shifted(padded, axis, 0)
        + 16.0 * shifted(padded, axis, 1)
        - 30.0 * shifted(padded, axis, 2)
        + 16.0 * shifted(padded, axis, 3)
        - shifted(padded, axis, 4)
    ) / 12.0


def remesh_padded(field, displace, axis):
    length = field.shape[axis] - 4
    total = jnp.zeros(field.shape[:axis] + (length,) + field.shape[axis + 1 :], jnp.float32)
    for offset in range(-2, 3):
        start = 2 - offset
        part = lax.slice_in_dim(field, start, start + length, axis=axis)
        moved = lax.slice_in_dim(displace, start, start + length, axis=axis - 1)
        total = total + remesh_kernel(offset - moved)[None] * part
    return total


def blade_forces(point_velocity, chord, twist, angle_step):
    count = point_velocity.shape[1]
    points = jnp.arange(count, dtype=jnp.int32)
    station = points % BP
    blade = points // BP % BLADES
    theta = angle_step[0].astype(
        jnp.float32
    ) * turn_step + 2.0 * 3.141592653589793 / 3.0 * blade.astype(jnp.float32)
    radius = (station.astype(jnp.float32) + 0.5) / BP
    cos_t = jnp.cos(theta)
    sin_t = jnp.sin(theta)
    rel_x = point_velocity[0]
    rel_y = point_velocity[1] + tip_speed * radius * sin_t
    rel_z = point_velocity[2] - tip_speed * radius * cos_t
    rel_t = -sin_t * rel_y + cos_t * rel_z
    speed = jnp.sqrt(rel_x * rel_x + rel_t * rel_t + 1.0)
    gamma = 3.141592653589793 * chord * (rel_x * jnp.cos(twist) + rel_t * jnp.sin(twist))
    blades = gamma.reshape(-1, BP)
    before = jnp.concatenate([jnp.zeros((blades.shape[0], 1), jnp.float32), blades[:, :-1]], axis=1)
    shed = (blades - before).reshape(-1)
    return jnp.stack(
        [
            shed * rel_x / speed,
            gamma * cos_t + shed * rel_y / speed,
            gamma * sin_t + shed * rel_z / speed,
        ]
    )


def point_tables(
    cells,
    fracs,
    owner_span,
    owner_vert,
    span_index,
    vert_index,
    span_cells,
    vert_cells,
    axial_cells,
):
    rows_x = jnp.arange(axial_cells, dtype=jnp.int32)
    rows_y = jnp.arange(span_cells, dtype=jnp.int32)
    rows_z = jnp.arange(vert_cells, dtype=jnp.int32)
    gap_x = rows_x[:, None] - cells[0][None, :]
    gap_y = (
        span_index * span_cells
        + rows_y[:, None]
        - owner_span[None, :] * span_cells
        - cells[1][None, :]
    )
    gap_z = (
        vert_index * vert_cells
        + rows_z[:, None]
        - owner_vert[None, :] * vert_cells
        - cells[2][None, :]
    )
    table_x = remesh_kernel(gap_x.astype(jnp.float32) - fracs[0][None, :])
    table_y = remesh_kernel(gap_y.astype(jnp.float32) - fracs[1][None, :])
    table_z = remesh_kernel(gap_z.astype(jnp.float32) - fracs[2][None, :])
    return (table_x, table_y, table_z)


def on_device(omega, velocity, point_owner, point_cells, point_frac, chord, twist, angle_step):
    span_cells, vert_cells, axial_cells = (omega.shape[1], omega.shape[2], omega.shape[3])
    span_count = lax.axis_size(GY)
    vert_count = lax.axis_size(GZ)
    span_index = lax.axis_index(GY)
    vert_index = lax.axis_index(GZ)
    owner_span = point_owner // vert_count
    owner_vert = point_owner % vert_count
    highest = lax.Precision.HIGHEST
    busiest = 2 * (BLADES * BP) // (span_count // TURBINES * max(vert_count // 2, 1))
    my_block = span_index * vert_count + vert_index
    points = jnp.arange(point_owner.shape[0], dtype=jnp.int32)
    ranking = jnp.where(point_owner == my_block, points, points + point_owner.shape[0])
    picked = jnp.argsort(ranking, stable=True)[:busiest]
    selector = (picked[:, None] == points[None, :]).astype(jnp.float32)
    table_x, table_y, table_z = point_tables(
        point_cells[:, picked],
        point_frac[:, picked],
        owner_span[picked],
        owner_vert[picked],
        span_index,
        vert_index,
        span_cells,
        vert_cells,
        axial_cells,
    )
    columns = jnp.dot(
        velocity.reshape(-1, axial_cells),
        table_x,
        precision=highest,
        preferred_element_type=jnp.float32,
    )
    columns = columns.reshape(3, span_cells, vert_cells, -1)
    compact = jnp.einsum("cyzq,yq,zq->cq", columns, table_y, table_z, precision=highest)
    partial_velocity = jnp.dot(
        compact, selector, precision=highest, preferred_element_type=jnp.float32
    )
    point_velocity = by_axis(partial_velocity, GY_GZ)
    sources = blade_forces(point_velocity, chord, twist, angle_step)
    local_sources = sources[:, picked]
    spread = jnp.einsum("cq,yq,zq->cyzq", local_sources, table_y, table_z, precision=highest)
    smear = jnp.dot(
        spread.reshape(-1, spread.shape[3]),
        table_x.T,
        precision=highest,
        preferred_element_type=jnp.float32,
    )
    smear = smear.reshape(3, span_cells, vert_cells, axial_cells)
    omega_rim, velocity_rim = (
        with_halo(omega, ((GY, 1), (GZ, 2)), 2),
        with_halo(velocity, ((GY, 1), (GZ, 2)), 2),
    )
    axial_pads = ((0, 0), (0, 0), (0, 0), (2, 2))
    omega_pad = jnp.pad(omega_rim, axial_pads)
    velocity_pad = jnp.pad(velocity_rim, axial_pads)
    stretch = jnp.zeros_like(omega)
    laplace = jnp.zeros_like(omega)
    for axis in range(3):
        stretch = stretch + omega[2 - axis][None] * centered_first(velocity_pad, 3 - axis)
        laplace = laplace + centered_second(omega_pad, axis + 1)
    section = omega + section_step * (stretch + viscosity * laplace + smear)
    shift_x = jnp.clip(section_step * velocity[0], -1.0, 1.0)
    moved_x = remesh_padded(
        jnp.pad(section, axial_pads), jnp.pad(shift_x, ((0, 0), (0, 0), (2, 2))), 3
    )
    shift_z = jnp.clip(section_step * velocity_rim[2][2 : span_cells + 2, :, :], -1.0, 1.0)
    span_rim = with_halo_2(moved_x, ((GY, 1),), 2)
    shift_y = jnp.clip(section_step * velocity_rim[1][:, 2 : vert_cells + 2, :], -1.0, 1.0)
    moved_mid = remesh_padded(span_rim, shift_y, 1)
    moved_y = with_halo_2(moved_mid, ((GZ, 2),), 2)
    omega_out = remesh_padded(moved_y, shift_z, 2)
    return (omega_out, sources)


def solution(mesh):
    split = Mesh(mesh.devices.reshape(8, 4, 2, 2, 4), ("gy_0", "gy_1", "gy_2", "gz_0", "gz_1"))
    placed = (P(None, GY, GZ, None), P(None, GY, GZ, None), P(), P(), P(), P(), P(), P())
    return jax.shard_map(
        on_device,
        mesh=split,
        in_specs=placed,
        out_specs=(P(None, GY, GZ, None), P()),
        check_vma=False,
    )
```

profile of v0, /device:TPU:96, one launch (start us, length us, event | category | flops | bytes accessed | tf_op | source)
XLA Modules:
  0.0 213.7 jit_solution(1090650749825777599)
XLA Ops:
  0.7 1.9 fusion.256
  2.6 1.9 collective-permute-start.1
  4.5 1.8 fusion.258
  6.3 2.7 %collective-permute-start.4 = (f32[3,2,64,128]{3,2,1,0:T(8,128)}, f32[3,2,64,128]{3,2,1,0:T(8,128)}, u32[]{:S(2)}, u32[]{:S(2)}) collective-permute-start(f32[3,2,64,128]{3,2,1,0:T(8,128)} %get-tuple-element.35), channel_id=1, source_target_pairs={{0,8},{8,16},{16,24},{24,32},{32,40},{40,48},{48,56},{56,64},{64,7... | collective-permute-start | bytes 589832 | tf_op jit(solution)/shard_map/ppermute | solution.py:35
  9.0 0.7 fusion.255
  9.7 3.4 %collective-permute-start = (f32[3,16,2,128]{3,2,1,0:T(2,128)}, f32[3,16,2,128]{3,2,1,0:T(2,128)}, u32[]{:S(2)}, u32[]{:S(2)}) collective-permute-start(f32[3,16,2,128]{3,2,1,0:T(2,128)} %get-tuple-element.28), channel_id=1, source_target_pairs={{0,1},{1,2},{2,3},{3,4},{4,5},{5,6},{6,7},{8,9},{9,10},{10,11},{11... | collective-permute-start | bytes 147464 | tf_op jit(solution)/shard_map/ppermute | solution.py:35
  13.1 8.5 %collective-permute-start.3 = (f32[3,16,2,128]{3,2,1,0:T(2,128)}, f32[3,16,2,128]{3,2,1,0:T(2,128)S(1)}, u32[]{:S(2)}, u32[]{:S(2)}) collective-permute-start(f32[3,16,2,128]{3,2,1,0:T(2,128)} %get-tuple-element.29), channel_id=1, source_target_pairs={{1,0},{2,1},{3,2},{4,3},{5,4},{6,5},{7,6},{9,8},{10,9},{11,10},{12... | collective-permute-start | bytes 147464 | tf_op jit(solution)/shard_map/ppermute | solution.py:36
  21.6 1.7 fusion.257
  23.3 1.9 collective-permute-start.6
  25.3 5.0 %sort.17 = (s32[1152]{0:T(1024)}, s32[1152]{0:T(1024)S(1)}) sort(s32[1152]{0:T(1024)S(1)} %get-tuple-element.61, s32[1152]{0:T(1024)S(1)} %iota.43), dimensions={0}, to_apply=%region_0.1 | sort | flops 12672 | bytes 18432 | tf_op jit(solution)/shard_map/jit(argsort)/sort | solution.py:184
  33.6 2.1 convolution_bitcast_fusion
  35.7 1.0 reshape.177
  36.7 0.7 gather_fusion
  37.5 0.7 fusion.234
  38.2 1.2 fusion.231
  39.7 0.9 fusion.172
  40.6 32.1 %psum.35 = f32[3,1152]{1,0:T(4,128)S(1)} all-reduce(f32[3,1152]{1,0:T(4,128)S(1)} %fusion.172), channel_id=1, replica_groups=mesh['gy_0'=8,'gy_1'=4,'gy_2'=2,'gz_0'=2,'gz_1'=4] {'gy_0'}, use_global_device_ids=true, to_apply=%region_1.2 | all-reduce | flops 3456 | bytes 27648 | tf_op jit(solution)/shard_map/psum | solution.py:23
  72.7 19.3 %psum.36 = f32[3,1152]{1,0:T(4,128)S(1)} all-reduce(f32[3,1152]{1,0:T(4,128)S(1)} %psum.35), channel_id=1, replica_groups=mesh['gy_0'=8,'gy_1'=4,'gy_2'=2,'gz_0'=2,'gz_1'=4] {'gy_1'}, use_global_device_ids=true, to_apply=%region_2.3 | all-reduce | flops 3456 | bytes 27648 | tf_op jit(solution)/shard_map/psum | solution.py:23
  91.9 3.4 %psum.37 = f32[3,1152]{1,0:T(4,128)S(1)} all-reduce(f32[3,1152]{1,0:T(4,128)S(1)} %psum.36), channel_id=1, replica_groups=mesh['gy_0'=8,'gy_1'=4,'gy_2'=2,'gz_0'=2,'gz_1'=4] {'gy_2'}, use_global_device_ids=true, to_apply=%region_3.4 | all-reduce | flops 3456 | bytes 27648 | tf_op jit(solution)/shard_map/psum | solution.py:23
  95.3 10.7 %psum.38 = f32[3,1152]{1,0:T(4,128)S(1)} all-reduce(f32[3,1152]{1,0:T(4,128)S(1)} %psum.37), channel_id=1, replica_groups=mesh['gy_0'=8,'gy_1'=4,'gy_2'=2,'gz_0'=2,'gz_1'=4] {'gz_0'}, use_global_device_ids=true, to_apply=%region_4.5 | all-reduce | flops 3456 | bytes 27648 | tf_op jit(solution)/shard_map/psum | solution.py:23
  106.1 22.9 %psum.39 = f32[3,1152]{1,0:T(4,128)S(1)} all-reduce(f32[3,1152]{1,0:T(4,128)S(1)} %psum.38), channel_id=1, replica_groups=mesh['gy_0'=8,'gy_1'=4,'gy_2'=2,'gz_0'=2,'gz_1'=4] {'gz_1'}, use_global_device_ids=true, to_apply=%region_5.6 | all-reduce | flops 3456 | bytes 27648 | tf_op jit(solution)/shard_map/psum | solution.py:23
  130.0 1.2 multiply_bitcast_fusion.2
  131.3 1.2 fusion.96
  132.8 2.6 %fusion.85 = (f32[16,64,128]{2,1,0:T(8,128)}, f32[16,64,128]{2,1,0:T(8,128)}, f32[16,64,128]{2,1,0:T(8,128)}, f32[16,64,128]{2,1,0:T(8,128)}) fusion(f32[16,64,128]{2,1,0:T(8,128)S(1)} %get-tuple-element.18), kind=kLoop, calls=%fused_computation.191 | loop fusion | flops 9437184 | bytes 2621440 | tf_op jit(solution)/shard_map/jit(_where)/select_n | solution.py:64
  135.4 1.1 copy.16
  136.4 1.6 gather_fusion.4
  138.2 1.9 collective-permute-start.7
  140.1 0.8 pad.29
  140.9 1.9 collective-permute-start.2
  142.9 3.3 %collective-permute-start.5 = (f32[3,2,64,128]{3,2,1,0:T(8,128)}, f32[3,2,64,128]{3,2,1,0:T(8,128)S(1)}, u32[]{:S(2)}, u32[]{:S(2)}) collective-permute-start(f32[3,2,64,128]{3,2,1,0:T(8,128)} %get-tuple-element.34), channel_id=1, source_target_pairs={{8,0},{16,8},{24,16},{32,24},{40,32},{48,40},{56,48},{64,56},{72,6... | collective-permute-start | bytes 589832 | tf_op jit(solution)/shard_map/ppermute | solution.py:36
  146.3 1.0 constant_dynamic-update-slice_fusion.4
  147.3 1.0 constant_dynamic-update-slice_fusion.8
  148.2 1.2 constant_dynamic-update-slice_fusion.3
  149.9 1.0 copy-done.5
  151.0 3.7 %select_maximum_fusion = f32[3,20,68,132]{3,2,1,0:T(8,128)} fusion(f32[3,20,2,128]{3,2,1,0:T(2,128)S(1)} %pad.34, f32[3,20,64,128]{3,2,1,0:T(8,128)S(1)} %get-tuple-element.57, f32[3,20,2,128]{3,2,1,0:T(2,128)S(1)} %pad.33), kind=kLoop, calls=%fused_computation.15 | loop fusion | flops 4308480 | bytes 4243200 | tf_op jit(solution)/shard_map/concatenate | solution.py:42
  154.8 19.1 %fusion.27 = f32[3,16,64,128]{3,2,1,0:T(8,128)} fusion(f32[3,16,64,128]{3,2,1,0:T(8,128)S(1)} %copy-done.1, f32[3,20,64,128]{3,2,1,0:T(8,128)} %copy-done.3, f32[3,20,2,128]{3,2,1,0:T(2,128)S(1)} %pad.34, f32[3,20,2,128]{3,2,1,0:T(2,128)S(1)} %pad.33, f32[3,20,64,128]{3,2,1,0:T(8,128)} %copy-done.2, f32[3,20,2,128]{3,2,1,0:T(2,128)S(1)} %pad.30, ...), kind=kOutput, calls=%fused_computation.66 | convolution fusion | flops 64931328 | bytes 29863944 | tf_op jit(solution)/shard_map/dot_general | solution.py:212
  173.9 6.4 %fusion.45 = f32[3,16,64,128]{3,2,1,0:T(8,128)S(1)} fusion(f32[3,16,64,128]{3,2,1,0:T(8,128)} %fusion.27, f32[16,64,128]{2,1,0:T(8,128)} %get-tuple-element.49, f32[16,64,128]{2,1,0:T(8,128)} %get-tuple-element.48, f32[16,64,128]{2,1,0:T(8,128)} %get-tuple-element.17, f32[16,64,128]{2,1,0:T(8,128)} %get-tuple-element.47, f32[16,64,128]{2,1,0:T(8,128)} %get-tuple-element.46), kind=kLoop, calls=%fused_computation.84 | loop fusion | flops 3538944 | bytes 5767168 | tf_op jit(solution)/shard_map/add | solution.py:105
  180.3 4.8 %collective-permute-start.8 = (f32[3,2,64,128]{3,2,1,0:T(8,128)S(1)}, f32[3,2,64,128]{3,2,1,0:T(8,128)S(1)}, u32[]{:S(2)}, u32[]{:S(2)}) collective-permute-start(f32[3,2,64,128]{3,2,1,0:T(8,128)S(1)} %get-tuple-element.15), channel_id=1, source_target_pairs={{8,0},{16,8},{24,16},{32,24},{40,32},{48,40},{56,48},{64,56},{72,6... | collective-permute-start | bytes 589832 | tf_op jit(solution)/shard_map/ppermute | solution.py:55
  185.1 1.9 collective-permute-start.9
  187.1 1.5 fusion.80
  188.8 1.2 collective-permute-done.8
  189.9 4.9 %collective-permute-done.9 = f32[3,2,64,128]{3,2,1,0:T(8,128)S(1)} collective-permute-done((f32[3,2,64,128]{3,2,1,0:T(8,128)S(1)}, f32[3,2,64,128]{3,2,1,0:T(8,128)S(1)}, u32[]{:S(2)}, u32[]{:S(2)}) %collective-permute-start.9) | collective-permute-done | bytes 196640 | tf_op jit(solution)/shard_map/ppermute | solution.py:54
  194.8 1.3 fusion.12
  196.2 3.4 %collective-permute-start.10 = (f32[3,16,2,128]{3,2,1,0:T(2,128)S(1)}, f32[3,16,2,128]{3,2,1,0:T(2,128)S(1)}, u32[]{:S(2)}, u32[]{:S(2)}) collective-permute-start(f32[3,16,2,128]{3,2,1,0:T(2,128)S(1)} %get-tuple-element.13), channel_id=1, source_target_pairs={{1,0},{2,1},{3,2},{4,3},{5,4},{6,5},{7,6},{9,8},{10,9},{11,10},{12... | collective-permute-start | bytes 147464 | tf_op jit(solution)/shard_map/ppermute | solution.py:55
  199.6 2.4 %collective-permute-start.11 = (f32[3,16,2,128]{3,2,1,0:T(2,128)S(1)}, f32[3,16,2,128]{3,2,1,0:T(2,128)S(1)}, u32[]{:S(2)}, u32[]{:S(2)}) collective-permute-start(f32[3,16,2,128]{3,2,1,0:T(2,128)S(1)} %get-tuple-element.14), channel_id=1, source_target_pairs={{0,1},{1,2},{2,3},{3,4},{4,5},{5,6},{6,7},{8,9},{9,10},{10,11},{11... | collective-permute-start | bytes 147464 | tf_op jit(solution)/shard_map/ppermute | solution.py:54
  202.0 1.7 fusion.75
  203.7 7.9 %collective-permute-done.11 = f32[3,16,2,128]{3,2,1,0:T(2,128)S(1)} collective-permute-done((f32[3,16,2,128]{3,2,1,0:T(2,128)S(1)}, f32[3,16,2,128]{3,2,1,0:T(2,128)S(1)}, u32[]{:S(2)}, u32[]{:S(2)}) %collective-permute-start.11) | collective-permute-done | bytes 49184 | tf_op jit(solution)/shard_map/ppermute | solution.py:54
  211.6 2.1 fusion.4
  (86 shorter events, 5.2 us)
Async XLA Ops:
  0.6 8.4 %copy-start = (f32[3,16,64,128]{3,2,1,0:T(8,128)S(1)}, f32[3,16,64,128]{3,2,1,0:T(8,128)}, u32[]{:S(2)}) copy-start(f32[3,16,64,128]{3,2,1,0:T(8,128)} %param.9) | copy-start | bytes 4718596
  0.6 24.6 %copy-start.15 = (s32[1152]{0:T(1024)S(1)}, s32[1152]{0:T(1024)}, u32[]{:S(2)}) copy-start(s32[1152]{0:T(1024)} %param.10) | copy-start | bytes 13828
  0.7 30.8 %copy-start.10 = (f32[3,1152]{1,0:T(4,128)S(1)}, f32[3,1152]{1,0:T(4,128)}, u32[]{:S(2)}) copy-start(f32[3,1152]{1,0:T(4,128)} %param.12) | copy-start | bytes 41476
  0.7 31.8 %copy-start.11 = (s32[3,1152]{1,0:T(4,128)S(1)}, s32[3,1152]{1,0:T(4,128)}, u32[]{:S(2)}) copy-start(s32[3,1152]{1,0:T(4,128)} %param.11) | copy-start | bytes 41476
  2.6 143.7 %collective-permute-start.1 = (f32[3,2,64,128]{3,2,1,0:T(8,128)}, f32[3,2,64,128]{3,2,1,0:T(8,128)}, u32[]{:S(2)}, u32[]{:S(2)}) collective-permute-start(f32[3,2,64,128]{3,2,1,0:T(8,128)} %get-tuple-element.31), channel_id=1, source_target_pairs={{0,8},{8,16},{16,24},{24,32},{32,40},{40,48},{48,56},{56,64},{64,7... | collective-permute-start | bytes 589832 | tf_op jit(solution)/shard_map/ppermute | solution.py:35
  6.3 140.9 %collective-permute-start.4 = (f32[3,2,64,128]{3,2,1,0:T(8,128)}, f32[3,2,64,128]{3,2,1,0:T(8,128)}, u32[]{:S(2)}, u32[]{:S(2)}) collective-permute-start(f32[3,2,64,128]{3,2,1,0:T(8,128)} %get-tuple-element.35), channel_id=1, source_target_pairs={{0,8},{8,16},{16,24},{24,32},{32,40},{40,48},{48,56},{56,64},{64,7... | collective-permute-start | bytes 589832 | tf_op jit(solution)/shard_map/ppermute | solution.py:35
  9.7 128.4 %collective-permute-start = (f32[3,16,2,128]{3,2,1,0:T(2,128)}, f32[3,16,2,128]{3,2,1,0:T(2,128)}, u32[]{:S(2)}, u32[]{:S(2)}) collective-permute-start(f32[3,16,2,128]{3,2,1,0:T(2,128)} %get-tuple-element.28), channel_id=1, source_target_pairs={{0,1},{1,2},{2,3},{3,4},{4,5},{5,6},{6,7},{8,9},{9,10},{10,11},{11... | collective-permute-start | bytes 147464 | tf_op jit(solution)/shard_map/ppermute | solution.py:35
  13.1 127.8 %collective-permute-start.3 = (f32[3,16,2,128]{3,2,1,0:T(2,128)}, f32[3,16,2,128]{3,2,1,0:T(2,128)S(1)}, u32[]{:S(2)}, u32[]{:S(2)}) collective-permute-start(f32[3,16,2,128]{3,2,1,0:T(2,128)} %get-tuple-element.29), channel_id=1, source_target_pairs={{1,0},{2,1},{3,2},{4,3},{5,4},{6,5},{7,6},{9,8},{10,9},{11,10},{12... | collective-permute-start | bytes 147464 | tf_op jit(solution)/shard_map/ppermute | solution.py:36
  23.3 119.6 %collective-permute-start.6 = (f32[3,16,2,128]{3,2,1,0:T(2,128)}, f32[3,16,2,128]{3,2,1,0:T(2,128)S(1)}, u32[]{:S(2)}, u32[]{:S(2)}) collective-permute-start(f32[3,16,2,128]{3,2,1,0:T(2,128)} %get-tuple-element.32), channel_id=1, source_target_pairs={{0,1},{1,2},{2,3},{3,4},{4,5},{5,6},{6,7},{8,9},{9,10},{10,11},{11... | collective-permute-start | bytes 147464 | tf_op jit(solution)/shard_map/ppermute | solution.py:35
  33.5 39.2 %copy-start.16 = (s32[9]{0:T(128)}, s32[9]{0:T(128)S(1)}, u32[]{:S(2)}) copy-start(s32[9]{0:T(128)S(1)} %get-tuple-element.7) | copy-start | bytes 112
  33.5 96.1 %copy-start.12 = (f32[1152]{0:T(1024)S(1)}, f32[1152]{0:T(1024)}, u32[]{:S(2)}) copy-start(f32[1152]{0:T(1024)} %param.14) | copy-start | bytes 13828
  33.5 96.1 %copy-start.13 = (f32[1152]{0:T(1024)S(1)}, f32[1152]{0:T(1024)}, u32[]{:S(2)}) copy-start(f32[1152]{0:T(1024)} %param.13) | copy-start | bytes 13828
  33.6 96.5 %copy-start.1 = (f32[3,16,64,128]{3,2,1,0:T(8,128)S(1)}, f32[3,16,64,128]{3,2,1,0:T(8,128)}, u32[]{:S(2)}) copy-start(f32[3,16,64,128]{3,2,1,0:T(8,128)} %param.8) | copy-start | bytes 4718596
  132.7 5.4 %copy-start.7 = (f32[3,16,2,128]{3,2,1,0:T(2,128)S(1)}, f32[3,16,2,128]{3,2,1,0:T(2,128)}, u32[]{:S(2)}) copy-start(f32[3,16,2,128]{3,2,1,0:T(2,128)} %get-tuple-element.33) | copy-start | bytes 147460
  135.4 14.1 %copy-start.6 = (f32[3,1152]{1,0:T(4,128)}, f32[3,1152]{1,0:T(4,128)S(1)}, u32[]{:S(2)}) copy-start(f32[3,1152]{1,0:T(4,128)S(1)} %pad_maximum_fusion.9) | copy-start | bytes 41476
  138.2 8.1 %collective-permute-start.7 = (f32[3,16,2,128]{3,2,1,0:T(2,128)S(1)}, f32[3,16,2,128]{3,2,1,0:T(2,128)S(1)}, u32[]{:S(2)}, u32[]{:S(2)}) collective-permute-start(f32[3,16,2,128]{3,2,1,0:T(2,128)S(1)} %copy-done.7), channel_id=1, source_target_pairs={{1,0},{2,1},{3,2},{4,3},{5,4},{6,5},{7,6},{9,8},{10,9},{11,10},{12... | collective-permute-start | bytes 147464 | tf_op jit(solution)/shard_map/ppermute | solution.py:36
  140.9 8.5 %collective-permute-start.2 = (f32[3,2,64,128]{3,2,1,0:T(8,128)}, f32[3,2,64,128]{3,2,1,0:T(8,128)S(1)}, u32[]{:S(2)}, u32[]{:S(2)}) collective-permute-start(f32[3,2,64,128]{3,2,1,0:T(8,128)} %get-tuple-element.30), channel_id=1, source_target_pairs={{8,0},{16,8},{24,16},{32,24},{40,32},{48,40},{56,48},{64,56},{72,6... | collective-permute-start | bytes 589832 | tf_op jit(solution)/shard_map/ppermute | solution.py:36
  142.9 8.0 %collective-permute-start.5 = (f32[3,2,64,128]{3,2,1,0:T(8,128)}, f32[3,2,64,128]{3,2,1,0:T(8,128)S(1)}, u32[]{:S(2)}, u32[]{:S(2)}) collective-permute-start(f32[3,2,64,128]{3,2,1,0:T(8,128)} %get-tuple-element.34), channel_id=1, source_target_pairs={{8,0},{16,8},{24,16},{32,24},{40,32},{48,40},{56,48},{64,56},{72,6... | collective-permute-start | bytes 589832 | tf_op jit(solution)/shard_map/ppermute | solution.py:36
  149.4 5.3 %copy-start.8 = (f32[3,18,64,128]{3,2,1,0:T(8,128)}, f32[3,18,64,128]{3,2,1,0:T(8,128)S(1)}, u32[]{:S(2)}) copy-start(f32[3,18,64,128]{3,2,1,0:T(8,128)S(1)} %get-tuple-element.22) | copy-start | bytes 5308420
  149.5 5.3 %copy-start.9 = (f32[3,18,64,128]{3,2,1,0:T(8,128)}, f32[3,18,64,128]{3,2,1,0:T(8,128)S(1)}, u32[]{:S(2)}) copy-start(f32[3,18,64,128]{3,2,1,0:T(8,128)S(1)} %get-tuple-element.71) | copy-start | bytes 5308420
  149.5 1.4 copy-start.5
  149.5 5.2 %copy-start.2 = (f32[3,20,64,128]{3,2,1,0:T(8,128)}, f32[3,20,64,128]{3,2,1,0:T(8,128)S(1)}, u32[]{:S(2)}) copy-start(f32[3,20,64,128]{3,2,1,0:T(8,128)S(1)} %get-tuple-element.53) | copy-start | bytes 5898244
  151.0 3.8 %copy-start.4 = (f32[3,18,64,128]{3,2,1,0:T(8,128)}, f32[3,18,64,128]{3,2,1,0:T(8,128)S(1)}, u32[]{:S(2)}) copy-start(f32[3,18,64,128]{3,2,1,0:T(8,128)S(1)} %get-tuple-element.56) | copy-start | bytes 5308420
  151.0 3.8 %copy-start.3 = (f32[3,20,64,128]{3,2,1,0:T(8,128)}, f32[3,20,64,128]{3,2,1,0:T(8,128)S(1)}, u32[]{:S(2)}) copy-start(f32[3,20,64,128]{3,2,1,0:T(8,128)S(1)} %get-tuple-element.57) | copy-start | bytes 5898244
  151.0 3.8 %copy-start.14 = (f32[9,64]{1,0:T(8,128)S(1)}, f32[9,64]{1,0:T(8,128)}, u32[]{:S(2)}) copy-start(f32[9,64]{1,0:T(8,128)} %get-tuple-element.68) | copy-start | bytes 6916
  151.0 3.8 %copy-start.17 = (s32[9]{0:T(128)S(1)}, s32[9]{0:T(128)}, u32[]{:S(2)}) copy-start(s32[9]{0:T(128)} %copy-done.16) | copy-start | bytes 112
  180.3 9.6 %collective-permute-start.8 = (f32[3,2,64,128]{3,2,1,0:T(8,128)S(1)}, f32[3,2,64,128]{3,2,1,0:T(8,128)S(1)}, u32[]{:S(2)}, u32[]{:S(2)}) collective-permute-start(f32[3,2,64,128]{3,2,1,0:T(8,128)S(1)} %get-tuple-element.15), channel_id=1, source_target_pairs={{8,0},{16,8},{24,16},{32,24},{40,32},{48,40},{56,48},{64,56},{72,6... | collective-permute-start | bytes 589832 | tf_op jit(solution)/shard_map/ppermute | solution.py:55
  185.1 9.7 %collective-permute-start.9 = (f32[3,2,64,128]{3,2,1,0:T(8,128)S(1)}, f32[3,2,64,128]{3,2,1,0:T(8,128)S(1)}, u32[]{:S(2)}, u32[]{:S(2)}) collective-permute-start(f32[3,2,64,128]{3,2,1,0:T(8,128)S(1)} %get-tuple-element.16), channel_id=1, source_target_pairs={{0,8},{8,16},{16,24},{24,32},{32,40},{40,48},{48,56},{56,64},{64,7... | collective-permute-start | bytes 589832 | tf_op jit(solution)/shard_map/ppermute | solution.py:54
  196.2 7.5 %collective-permute-start.10 = (f32[3,16,2,128]{3,2,1,0:T(2,128)S(1)}, f32[3,16,2,128]{3,2,1,0:T(2,128)S(1)}, u32[]{:S(2)}, u32[]{:S(2)}) collective-permute-start(f32[3,16,2,128]{3,2,1,0:T(2,128)S(1)} %get-tuple-element.13), channel_id=1, source_target_pairs={{1,0},{2,1},{3,2},{4,3},{5,4},{6,5},{7,6},{9,8},{10,9},{11,10},{12... | collective-permute-start | bytes 147464 | tf_op jit(solution)/shard_map/ppermute | solution.py:55
  199.6 12.0 %collective-permute-start.11 = (f32[3,16,2,128]{3,2,1,0:T(2,128)S(1)}, f32[3,16,2,128]{3,2,1,0:T(2,128)S(1)}, u32[]{:S(2)}, u32[]{:S(2)}) collective-permute-start(f32[3,16,2,128]{3,2,1,0:T(2,128)S(1)} %get-tuple-element.14), channel_id=1, source_target_pairs={{0,1},{1,2},{2,3},{3,4},{4,5},{5,6},{6,7},{8,9},{9,10},{10,11},{11... | collective-permute-start | bytes 147464 | tf_op jit(solution)/shard_map/ppermute | solution.py:54
where the time goes:
time: 214 us
  blocking collectives  88.4 us (41%)
  starting transfers between devices  38 us (18%)
  other arithmetic  29.1 us (14%)
  matrix products  23.5 us (11%)
  local copies, waits for them, and re-layouts  18.8 us (9%)
  waiting for transfers between devices  13.9 us (6%)
    psum x5, blocking collectives, by_axis(): x = lax.psum(x, axis)  88.4 us
    dot_general x1, matrix products, on_device(): jnp.dot(spread.reshape(-1, spread.shape[3]), table_x.T, precision=highest...  19.1 us
    ppermute x4, starting transfers between devices, with_halo(): lax.ppermute(initial, axis, [(b, a) for a, b in up])  15.6 us
    ppermute x2, waiting for transfers between devices, with_halo_2(): before = lax.ppermute(last, axis, up)  12.7 us
    ppermute x4, starting transfers between devices, with_halo(): lax.ppermute(last, axis, up)  9.88 us
    add x3, other arithmetic, remesh_padded(): total = total + remesh_kernel(offset - moved)[None] * part  9.84 us
    ppermute x2, starting transfers between devices, with_halo_2(): after = lax.ppermute(initial, axis, down)  8.16 us
    select_n x5, other arithmetic, remesh_kernel(): return jnp.where(mag < 1.0, inner, jnp.where(mag < 2.0, outer, 0.0))  6.53 us
  transfers between devices with their start and end apart: 12, of which 3 were waited for; matrix products, arithmetic and copies ran while one was open for 17% of the time, Pallas kernels for 0%

commit v1 on v0

v1 whole, which is shorter than its diff:
```python
import functools

import jax
import jax.numpy as jnp
from jax import lax
from jax.experimental import pallas as pl
from jax.experimental.pallas import tpu as pltpu
from jax.sharding import PartitionSpec as P

TURBINES = 6
BLADES = 3
BP = 64
MESH = pl.DeviceIdType.MESH
HI = lax.Precision.HIGHEST

section_step = 0.4
viscosity = 0.05
tip_speed = 3.0
turn_step = 2.0 * 3.141592653589793 / 720.0
F32 = jnp.float32
BF = jnp.bfloat16

CHUNK = 32


def m4(shift):
    mag = jnp.abs(shift)
    inner = 1.0 + mag * mag * (1.5 * mag - 2.5)
    far = 2.0 - mag
    outer = 0.5 * far * far * (1.0 - mag)
    return jnp.where(mag < 1.0, inner, jnp.where(mag < 2.0, outer, 0.0))


def remesh_weights(v):
    a = jnp.minimum(section_step * jnp.abs(v), 1.0)
    b = 1.0 - a
    a2 = a * a
    b2 = b * b
    w0 = 1.0 + a2 * (1.5 * a - 2.5)
    w1 = 1.0 + b2 * (1.5 * b - 2.5)
    wm = -0.5 * a * b2
    w2 = -0.5 * a2 * b
    pos = v > 0.0
    return (
        jnp.where(pos, 0.0, w2),
        jnp.where(pos, wm, w1),
        w0,
        jnp.where(pos, w1, wm),
        jnp.where(pos, w2, 0.0),
    )


def split(x):
    hi = x.astype(BF)
    return hi, (x - hi.astype(F32)).astype(BF)


def dot3(a, b, dims):
    ah, al = a
    bh, bl = b
    dn = (dims, ((), ()))
    d = functools.partial(lax.dot_general, dimension_numbers=dn, preferred_element_type=F32)
    return d(ah, bh) + d(al, bh) + d(ah, bl)


def kernel(
    n_y, n_z,
    om_hbm, ve_hbm, own_ref, cell_ref, frac_ref, chord_ref, twist_ref, ang_ref,
    out_hbm, src_out,
    vb, wb, sb, mb, yb, wx, wy, wz, zs, zr, ks, kr, ob,
    vals, sel, pk, p1r, p2s, p2r, p3s, p3r, pvb, srcb, ab,
    ld_sem, ys, yr, zss, zsr, p1s, p1v, p2ss, p2v, p3ss, p3v, ms, mr, kss, ksr, osem,
):
    gy = lax.axis_index("gy")
    gz = lax.axis_index("gz")
    CY, CZ, NX = om_hbm.shape[1], om_hbm.shape[2], om_hbm.shape[3]
    span = n_y // TURBINES
    nvb = max(n_z // 2, 1)
    vb0 = (n_z - nvb) // 2
    NS = span * TURBINES
    zc = gy // 8
    plane = gy % 8
    t_own = jnp.minimum(gy // span, TURBINES - 1)
    rb = (3 * t_own) // 2
    n_zc = n_y // 8
    has_dn, has_up = gy > 0, gy < n_y - 1
    has_l, has_r = gz > 0, gz < n_z - 1
    in_span = gy < NS
    is_src = in_span & (gz >= vb0) & (gz < vb0 + nvb)

    bar = pltpu.get_barrier_semaphore()
    for d in range(1, n_z):
        pl.semaphore_signal(bar, inc=1, device_id=(gy, lax.rem(gz + d, n_z)), device_id_type=MESH)
    for d in range(1, 8):
        pl.semaphore_signal(
            bar, inc=1, device_id=(zc * 8 + lax.rem(plane + d, 8), gz), device_id_type=MESH)
    for d in range(1, n_zc):
        pl.semaphore_signal(
            bar, inc=1, device_id=(lax.rem(zc + d, n_zc) * 8 + plane, gz), device_id_type=MESH)
    n_bar = (n_z - 1) + 7 + (n_zc - 1)
    cross_dn = has_dn & (plane == 0)
    cross_up = has_up & (plane == 7)

    @pl.when(cross_dn)
    def _():
        pl.semaphore_signal(bar, inc=1, device_id=(gy - 1, gz), device_id_type=MESH)

    @pl.when(cross_up)
    def _():
        pl.semaphore_signal(bar, inc=1, device_id=(gy + 1, gz), device_id_type=MESH)

    loads = []
    for c in range(3):
        loads.append(pltpu.make_async_copy(
            ve_hbm.at[c], vb.at[c, pl.ds(2, CY), pl.ds(8, CZ)], ld_sem.at[c]))
        loads.append(pltpu.make_async_copy(
            om_hbm.at[c], wb.at[c, pl.ds(2, CY), pl.ds(8, CZ)], ld_sem.at[3 + c]))
    for cp in loads:
        cp.start()

    ztile = jnp.zeros((8, NX), F32)

    def zfill(i, carry):
        for c in range(3):
            for buf in (vb, wb):
                buf[c, i + 2, pl.ds(0, 8), :] = ztile
                buf[c, i + 2, pl.ds(8 + CZ, 8), :] = ztile
            yb[c, i, pl.ds(0, 8), :] = ztile
            yb[c, i, pl.ds(8 + CZ, 8), :] = ztile
        return carry

    lax.fori_loop(0, CY, zfill, 0)

    def zero_y(lo):
        zrow = jnp.zeros((CZ, NX), F32)
        for c in range(3):
            for k in range(2):
                vb[c, lo + k, pl.ds(8, CZ), :] = zrow
                wb[c, lo + k, pl.ds(8, CZ), :] = zrow
                mb[c, lo + k] = zrow

    @pl.when(jnp.logical_not(has_dn))
    def _():
        zero_y(0)

    @pl.when(jnp.logical_not(has_up))
    def _():
        zero_y(CY + 2)

    @pl.when((zc + 1) * 8 > NS)
    def _():
        for s in range(8):
            @pl.when(zc * 8 + s >= NS)
            def _():
                p2r[s] = ztile

    vals[0:3, :] = cell_ref[...].astype(F32)
    vals[3:6, :] = frac_ref[...]
    my_block = gy * n_z + gz
    row8 = lax.broadcasted_iota(jnp.int32, (8, 128), 0)
    lane = lax.broadcasted_iota(jnp.int32, (8, 128), 1)
    ln128 = lax.broadcasted_iota(jnp.int32, (128, 128), 1)
    sb128 = lax.broadcasted_iota(jnp.int32, (128, 128), 0)
    base0 = pl.multiple_of(rb * 128, 128)
    base1 = pl.multiple_of(rb * 128 + 128, 128)
    o0 = jnp.broadcast_to(own_ref[:, pl.ds(base0, 128)], (8, 128))
    o1 = jnp.broadcast_to(own_ref[:, pl.ds(base1, 128)], (8, 128))
    own = jnp.where(row8 == 0, o0, jnp.where(row8 == 1, o1, -1))
    mine = own == my_block
    mf = mine.astype(F32)
    upper = (sb128 <= ln128).astype(F32)
    csum = jnp.dot(mf, upper, preferred_element_type=F32)
    tot0 = jnp.broadcast_to(csum[0:1, 127:128], (8, 128))
    rank = csum - mf + jnp.where(row8 == 1, tot0, 0.0)
    rank = jnp.where(mine, rank, -1.0)
    rank_t = jnp.transpose(jnp.concatenate([rank] * 16, axis=0))
    lanef = ln128.astype(F32)
    s0 = (jnp.broadcast_to(rank_t[:, 0:1], (128, 128)) == lanef).astype(F32)
    s1 = (jnp.broadcast_to(rank_t[:, 1:2], (128, 128)) == lanef).astype(F32)
    par = jnp.dot(vals[:, pl.ds(base0, 128)], s0, precision=HI, preferred_element_type=F32)
    par = par + jnp.dot(vals[:, pl.ds(base1, 128)], s1, precision=HI, preferred_element_type=F32)
    sel[0] = s0
    sel[1] = s1

    def table(n, k):
        rows = lax.broadcasted_iota(jnp.int32, (n, 128), 0).astype(F32)
        return m4((rows - par[k:k + 1, :]) - par[3 + k:4 + k, :])

    tx = table(NX, 0)
    tyq = table(CY, 1)
    tzq = table(CZ, 2)
    txs = split(tx)

    for cp in loads:
        cp.wait()

    def pack(i, carry):
        c = i // 4
        g = i % 4
        for f, buf in ((0, vb), (1, wb)):
            for j in range(4):
                y = 2 + 4 * g + j
                zs[0, f, c, g, 2 * j:2 * j + 2, :] = buf[c, y, 6 + CZ:8 + CZ, :]
                zs[1, f, c, g, 2 * j:2 * j + 2, :] = buf[c, y, 8:10, :]
        return carry

    lax.fori_loop(0, 12, pack, 0)

    pl.semaphore_wait(bar, n_bar + cross_dn.astype(jnp.int32) + cross_up.astype(jnp.int32))

    def rcopy(src, dst, ss, rs, dev):
        return pltpu.make_async_remote_copy(
            src_ref=src, dst_ref=dst, send_sem=ss, recv_sem=rs, device_id=dev, device_id_type=MESH)

    def z_copy(d):
        return rcopy(zs.at[d], zr.at[d], zss.at[d], zsr.at[d], (gy, gz + (1 if d == 0 else -1)))

    def y_copy(f, d):
        buf = vb if f == 0 else wb
        src, dst = (CY, 0) if d == 0 else (2, CY + 2)
        return rcopy(
            buf.at[:, pl.ds(src, 2), pl.ds(8, CZ)], buf.at[:, pl.ds(dst, 2), pl.ds(8, CZ)],
            ys.at[f, d], yr.at[f, d], (gy + (1 if d == 0 else -1), gz))

    up_cond = ((has_up, has_dn), (has_dn, has_up))
    rt_cond = ((has_r, has_l), (has_l, has_r))
    for d in range(2):
        @pl.when(rt_cond[d][0])
        def _():
            z_copy(d).start()

    for f in range(2):
        for d in range(2):
            @pl.when(up_cond[d][0])
            def _():
                y_copy(f, d).start()

    def sample(y, acc):
        wyr = tyq_row(y)
        out = []
        for c in range(3):
            v = split(vb[c, y + 2, pl.ds(8, CZ), :])
            col = dot3(v, txs, ((1,), (0,))) * tzq
            s = jnp.sum(col, axis=0, keepdims=True)
            out.append(acc[c] + s * wyr)
        return tuple(out)

    ab[0] = tyq

    def tyq_row(y):
        return ab[0, pl.ds(y, 1), :]

    zrow1 = jnp.zeros((1, 128), F32)
    pvq = lax.fori_loop(0, CY, sample, (zrow1, zrow1, zrow1))
    qa = jnp.zeros((8, 128), F32)
    qb = qa
    for c in range(3):
        full = jnp.broadcast_to(pvq[c], (8, 128))
        qa = jnp.where(row8 == c, full, qa)
        qb = jnp.where(row8 == c + 4, full, qb)
    dnt = (((1,), (1,)), ((), ()))
    packet = lax.dot_general(qa, s0, dnt, precision=HI, preferred_element_type=F32)
    packet = packet + lax.dot_general(qb, s1, dnt, precision=HI, preferred_element_type=F32)

    def p1_copy(d):
        return rcopy(pk, p1r.at[gz - vb0], p1s.at[d - 1], p1v.at[gz - vb0],
                     (gy, lax.rem(gz + d, n_z)))

    @pl.when(is_src)
    def _():
        pk[...] = packet
        p1r[gz - vb0] = packet
        for d in range(1, n_z):
            p1_copy(d).start()

    lanes = lax.broadcasted_iota(jnp.int32, (CHUNK, NX), 1)

    def wx_loop(y, carry):
        for z0 in range(0, CZ, CHUNK):
            w = remesh_weights(vb[0, y + 2, pl.ds(8 + z0, CHUNK), :])
            for k in range(5):
                s = k - 2
                x = w[k]
                if s > 0:
                    x = jnp.where(lanes < NX - s, x, 0.0)
                elif s < 0:
                    x = jnp.where(lanes >= -s, x, 0.0)
                wx[k, y, pl.ds(z0, CHUNK), :] = x
        return carry

    lax.fori_loop(0, CY, wx_loop, 0)

    def p1_wait(s):
        return rcopy(p1r.at[s], p1r.at[s], p1s.at[0], p1v.at[s], (gy, gz))

    @pl.when(in_span)
    def _():
        for s in range(nvb):
            @pl.when(gz != vb0 + s)
            def _():
                p1_wait(s).wait_recv()
        tile = p1r[0]
        for s in range(1, nvb):
            tile = tile + p1r[s]
        p2s[...] = tile
        p2r[plane] = tile

    def p2_copy(d):
        return rcopy(p2s, p2r.at[plane], p2ss.at[d - 1], p2v.at[plane],
                     (zc * 8 + lax.rem(plane + d, 8), gz))

    @pl.when(in_span)
    def _():
        for d in range(1, 8):
            p2_copy(d).start()

    def wz_loop(y, carry):
        for z0 in range(0, CZ, CHUNK):
            w = remesh_weights(vb[2, y + 2, pl.ds(8 + z0, CHUNK), :])
            for k in range(5):
                wz[k, y, pl.ds(8 + z0, CHUNK), :] = w[k]
        return carry

    lax.fori_loop(0, CY, wz_loop, 0)

    def wy_one(y):
        for z0 in range(0, CZ, CHUNK):
            w = remesh_weights(vb[1, y, pl.ds(8 + z0, CHUNK), :])
            for k in range(5):
                wy[k, y, pl.ds(z0, CHUNK), :] = w[k]

    def wy_loop(y, carry):
        wy_one(y + 2)
        return carry

    lax.fori_loop(0, CY, wy_loop, 0)

    for s in range(8):
        @pl.when((plane != s) & (zc * 8 + s < NS))
        def _():
            rcopy(p2r.at[s], p2r.at[s], p2ss.at[0], p2v.at[s], (gy, gz)).wait_recv()

    t_a = (zc * 8) // span
    suma = jnp.zeros((8, 128), F32)
    sumb = suma
    for s in range(8):
        x = p2r[s]
        first = (zc * 8 + s) // span == t_a
        suma = suma + jnp.where(first, x, 0.0)
        sumb = sumb + jnp.where(first, 0.0, x)
    p3s[0] = suma
    p3s[1] = sumb
    p3r[zc, 0] = suma
    p3r[zc, 1] = sumb

    def p3_copy(d):
        return rcopy(p3s, p3r.at[zc], p3ss.at[d - 1], p3v.at[zc],
                     (lax.rem(zc + d, n_zc) * 8 + plane, gz))

    for d in range(1, n_zc):
        p3_copy(d).start()

    for d in range(2):
        @pl.when(rt_cond[d][1])
        def _():
            z_copy(d).wait_recv()
            lo = 6 if d == 0 else 8 + CZ

            def unpack(i, carry):
                c = i // 4
                g = i % 4
                for f, buf in ((0, vb), (1, wb)):
                    for j in range(4):
                        buf[c, 2 + 4 * g + j, lo:lo + 2, :] = zr[d, f, c, g, 2 * j:2 * j + 2, :]
                return carry

            lax.fori_loop(0, 12, unpack, 0)

    def wz_edge(y, carry):
        for r0 in (0, 8 + CZ):
            w = remesh_weights(vb[2, y + 2, pl.ds(r0, 8), :])
            for k in range(5):
                wz[k, y, pl.ds(r0, 8), :] = w[k]
        return carry

    lax.fori_loop(0, CY, wz_edge, 0)

    for f in range(2):
        for d in range(2):
            @pl.when(up_cond[d][1])
            def _():
                y_copy(f, d).wait_recv()

    for y in (0, 1, CY + 2, CY + 3):
        wy_one(y)

    c0 = section_step / 12.0
    cl = section_step * viscosity / 12.0

    def around(buf, c, y, z0, dim):
        if dim == 2:
            return [buf[c, y + 2 + k, pl.ds(8 + z0, CHUNK), :] for k in (-2, -1, 1, 2)]
        if dim == 1:
            return [buf[c, y + 2, pl.ds(8 + z0 + k, CHUNK), :] for k in (-2, -1, 1, 2)]
        f = buf[c, y + 2, pl.ds(8 + z0, CHUNK), :]
        res = []
        for k in (-2, -1, 1, 2):
            r = pltpu.roll(f, (-k) % NX, 1)
            m = lanes >= -k if k < 0 else lanes < NX - k
            res.append(jnp.where(m, r, 0.0))
        return res

    def section_loop(y, carry):
        for z0 in range(0, CZ, CHUNK):
            om = [wb[c, y + 2, pl.ds(8 + z0, CHUNK), :] for c in range(3)]
            oms = [c0 * o for o in om]
            for c in range(3):
                acc = om[c]
                near = None
                far = None
                for dim in range(3):
                    a = around(vb, c, y, z0, dim)
                    acc = acc + oms[2 - dim] * (8.0 * (a[2] - a[1]) - (a[3] - a[0]))
                    b = around(wb, c, y, z0, dim)
                    n = b[1] + b[2]
                    e = b[0] + b[3]
                    near = n if near is None else near + n
                    far = e if far is None else far + e
                acc = acc + cl * (16.0 * near - far - 90.0 * om[c])
                sb[c, y, pl.ds(z0, CHUNK), :] = acc
        return carry

    lax.fori_loop(0, CY, section_loop, 0)

    for s in range(n_zc):
        @pl.when(zc != s)
        def _():
            rcopy(p3r.at[s], p3r.at[s], p3ss.at[0], p3v.at[s], (gy, gz)).wait_recv()

    tiles = [jnp.zeros((8, 128), F32) for _ in range(TURBINES)]
    for s in range(n_zc):
        ta = (s * 8) // span
        if ta < TURBINES:
            tiles[ta] = tiles[ta] + p3r[s, 0]
        if ta + 1 < TURBINES:
            tiles[ta + 1] = tiles[ta + 1] + p3r[s, 1]
    for u in range(TURBINES // 2):
        e, o = tiles[2 * u], tiles[2 * u + 1]
        for c in range(3):
            pvb[c, 3 * u:3 * u + 1, :] = e[c:c + 1]
            pvb[c, 3 * u + 1:3 * u + 2, :] = e[4 + c:5 + c] + o[c:c + 1]
            pvb[c, 3 * u + 2:3 * u + 3, :] = o[4 + c:5 + c]
    n_rows = TURBINES * BLADES * BP // 128
    for r in range(n_rows):
        pvb[3, r:r + 1, :] = chord_ref[:, 128 * r:128 * r + 128]
        pvb[4, r:r + 1, :] = twist_ref[:, 128 * r:128 * r + 128]
    r16 = lax.broadcasted_iota(jnp.int32, (16, 128), 0)
    l16 = lax.broadcasted_iota(jnp.int32, (16, 128), 1)
    live = r16 < n_rows
    station = l16 % BP
    blade = (2 * r16 + l16 // BP) % BLADES
    theta = ang_ref[0].astype(F32) * turn_step + 2.0 * 3.141592653589793 / 3.0 * blade.astype(F32)
    radius = (station.astype(F32) + 0.5) / BP
    cos_t = jnp.cos(theta)
    sin_t = jnp.sin(theta)
    chord = jnp.where(live, pvb[3], 0.0)
    twist = jnp.where(live, pvb[4], 0.0)
    rel_x = jnp.where(live, pvb[0], 0.0)
    rel_y = jnp.where(live, pvb[1], 0.0) + tip_speed * radius * sin_t
    rel_z = jnp.where(live, pvb[2], 0.0) - tip_speed * radius * cos_t
    rel_t = -sin_t * rel_y + cos_t * rel_z
    speed = jnp.sqrt(rel_x * rel_x + rel_t * rel_t + 1.0)
    gamma = 3.141592653589793 * chord * (rel_x * jnp.cos(twist) + rel_t * jnp.sin(twist))
    before = jnp.where(station == 0, 0.0, pltpu.roll(gamma, 1, 1))
    ratio = (gamma - before) / speed
    src = [ratio * rel_x, gamma * cos_t + ratio * rel_y, gamma * sin_t + ratio * rel_z]
    for r in range(n_rows):
        srcb[r, 3:8, :] = jnp.zeros((5, 128), F32)
        for c in range(3):
            src_out[c:c + 1, 128 * r:128 * r + 128] = src[c][r:r + 1]
            srcb[r, c:c + 1, :] = src[c][r:r + 1]
    srcq = jnp.dot(srcb[rb], sel[0], precision=HI, preferred_element_type=F32)
    srcq = srcq + jnp.dot(srcb[rb + 1], sel[1], precision=HI, preferred_element_type=F32)
    tyq2 = ab[0]
    for c in range(3):
        ab[c + 1] = section_step * tyq2 * srcq[c:c + 1, :]

    def move_x(y):
        for c in range(3):
            lhs = split(tzq * ab[c + 1, pl.ds(y, 1), :])
            smear = dot3(lhs, txs, ((1,), (1,)))
            f_all = sb[c, y] + smear
            for z0 in range(0, CZ, CHUNK):
                f = f_all[z0:z0 + CHUNK]
                g = wx[2, y, pl.ds(z0, CHUNK), :] * f
                for k in (0, 1, 3, 4):
                    p = wx[k, y, pl.ds(z0, CHUNK), :] * f
                    g = g + pltpu.roll(p, (k - 2) % NX, 1)
                mb[c, y + 2, pl.ds(z0, CHUNK), :] = g

    def edge_loop(i, carry):
        move_x(jnp.where(i < 2, i, i + CY - 4))
        return carry

    lax.fori_loop(0, 4, edge_loop, 0)

    def m_copy(d):
        src_y, dst_y = (CY, 0) if d == 0 else (2, CY + 2)
        return rcopy(mb.at[:, pl.ds(src_y, 2)], mb.at[:, pl.ds(dst_y, 2)],
                     ms.at[d], mr.at[d], (gy + (1 if d == 0 else -1), gz))

    for d in range(2):
        @pl.when(up_cond[d][0])
        def _():
            m_copy(d).start()

    def mid_loop(i, carry):
        move_x(i + 2)
        return carry

    lax.fori_loop(0, CY - 4, mid_loop, 0)

    def move_y(y):
        for z0 in range(0, CZ, CHUNK):
            w = [wy[k, y + 4 - k, pl.ds(z0, CHUNK), :] for k in range(5)]
            for c in range(3):
                g = w[0] * mb[c, y + 4, pl.ds(z0, CHUNK), :]
                for k in range(1, 5):
                    g = g + w[k] * mb[c, y + 4 - k, pl.ds(z0, CHUNK), :]
                yb[c, y, pl.ds(8 + z0, CHUNK), :] = g

    def mid_y(i, carry):
        move_y(i + 2)
        return carry

    lax.fori_loop(0, CY - 4, mid_y, 0)
    for d in range(2):
        @pl.when(up_cond[d][1])
        def _():
            m_copy(d).wait_recv()

    def edge_y(i, carry):
        move_y(jnp.where(i < 2, i, i + CY - 4))
        return carry

    lax.fori_loop(0, 4, edge_y, 0)

    def pack2(i, carry):
        c = i // 4
        g = i % 4
        for j in range(4):
            y = 4 * g + j
            ks[0, c, g, 2 * j:2 * j + 2, :] = yb[c, y, 6 + CZ:8 + CZ, :]
            ks[1, c, g, 2 * j:2 * j + 2, :] = yb[c, y, 8:10, :]
        return carry

    lax.fori_loop(0, 12, pack2, 0)

    def k_copy(d):
        return rcopy(ks.at[d], kr.at[d], kss.at[d], ksr.at[d], (gy, gz + (1 if d == 0 else -1)))

    for d in range(2):
        @pl.when(rt_cond[d][0])
        def _():
            k_copy(d).start()
    for d in range(2):
        @pl.when(rt_cond[d][1])
        def _():
            k_copy(d).wait_recv()
            lo = 6 if d == 0 else 8 + CZ

            def unpack2(i, carry):
                c = i // 4
                g = i % 4
                for j in range(4):
                    yb[c, 4 * g + j, lo:lo + 2, :] = kr[d, c, g, 2 * j:2 * j + 2, :]
                return carry

            lax.fori_loop(0, 12, unpack2, 0)

    def move_z(y, carry):
        for z0 in range(0, CZ, CHUNK):
            w = [wz[k, y, pl.ds(8 + z0 + 2 - k, CHUNK), :] for k in range(5)]
            for c in range(3):
                g = w[0] * yb[c, y, pl.ds(8 + z0 + 2, CHUNK), :]
                for k in range(1, 5):
                    g = g + w[k] * yb[c, y, pl.ds(8 + z0 + 2 - k, CHUNK), :]
                ob[c, y, pl.ds(z0, CHUNK), :] = g
        return carry

    lax.fori_loop(0, CY, move_z, 0)
    oc = pltpu.make_async_copy(ob, out_hbm, osem)
    oc.start()

    for d in range(2):
        @pl.when(rt_cond[d][0])
        def _():
            z_copy(d).wait_send()
            k_copy(d).wait_send()

        @pl.when(up_cond[d][0])
        def _():
            y_copy(0, d).wait_send()
            y_copy(1, d).wait_send()
            m_copy(d).wait_send()

    @pl.when(is_src)
    def _():
        for d in range(1, n_z):
            p1_copy(d).wait_send()

    @pl.when(in_span)
    def _():
        for d in range(1, 8):
            p2_copy(d).wait_send()

    for d in range(1, n_zc):
        p3_copy(d).wait_send()
    oc.wait()


def on_device(n_y, n_z, omega, velocity, owner, cells, frac, chord, twist, angle):
    _, cy, cz, nx = omega.shape
    n_p = owner.shape[0]
    n_zc = n_y // 8
    vm = pl.BlockSpec(memory_space=pltpu.VMEM)
    hb = pl.BlockSpec(memory_space=pl.ANY)
    sm = pl.BlockSpec(memory_space=pltpu.SMEM)
    nvb = max(n_z // 2, 1)
    V = pltpu.VMEM
    D = pltpu.SemaphoreType.DMA
    scratch = [
        V((3, cy + 4, cz + 16, nx), F32),
        V((3, cy + 4, cz + 16, nx), F32),
        V((3, cy, cz, nx), F32),
        V((3, cy + 4, cz, nx), F32),
        V((3, cy, cz + 16, nx), F32),
        V((5, cy, cz, nx), F32),
        V((5, cy + 4, cz, nx), F32),
        V((5, cy, cz + 16, nx), F32),
        V((2, 2, 3, cy // 4, 8, nx), F32),
        V((2, 2, 3, cy // 4, 8, nx), F32),
        V((2, 3, cy // 4, 8, nx), F32),
        V((2, 3, cy // 4, 8, nx), F32),
        V((3, cy, cz, nx), F32),
        V((8, n_p), F32),
        V((2, 128, 128), F32),
        V((8, 128), F32),
        V((nvb, 8, 128), F32),
        V((8, 128), F32),
        V((8, 8, 128), F32),
        V((2, 8, 128), F32),
        V((n_zc, 2, 8, 128), F32),
        V((5, 16, 128), F32),
        V((n_p // 128, 8, 128), F32),
        V((4, cy, 128), F32),
        D((6,)), D((2, 2)), D((2, 2)), D((2,)), D((2,)),
        D((n_z - 1,)), D((nvb,)), D((7,)), D((8,)), D((n_zc - 1,)), D((n_zc,)),
        D((2,)), D((2,)), D((2,)), D((2,)), D(()),
    ]
    out, src = pl.pallas_call(
        functools.partial(kernel, n_y, n_z),
        name="section",
        out_shape=(
            jax.ShapeDtypeStruct(omega.shape, F32),
            jax.ShapeDtypeStruct((3, n_p), F32),
        ),
        in_specs=[hb, hb, vm, vm, vm, vm, vm, sm],
        out_specs=(hb, vm),
        scratch_shapes=scratch,
        compiler_params=pltpu.CompilerParams(
            collective_id=0, has_side_effects=True, vmem_limit_bytes=60 * 1024 * 1024),
    )(omega, velocity, owner.reshape(1, n_p), cells, frac,
      chord.reshape(1, n_p), twist.reshape(1, n_p), angle)
    return out, src


def solution(mesh):
    n_y, n_z = mesh.shape["gy"], mesh.shape["gz"]
    field = P(None, "gy", "gz", None)
    return jax.shard_map(
        functools.partial(on_device, n_y, n_z),
        mesh=mesh,
        in_specs=(field, field, P(), P(), P(), P(), P(), P()),
        out_specs=(field, P()),
        check_vma=False,
    )
```

time: 214 us -> 65.9 us (0.31)
  the two profiles are of different devices: /device:TPU:96 before, /device:TPU:23 now
where the time goes in v1:
time: 65.9 us; the launch traced here: 65.5 us
  Pallas kernels  57 us (86%)
  local copies, waits for them, and re-layouts  7.22 us (11%)
  between operations  1.3 us (2%)
    pallas_call x1, Pallas kernels, on_device(): pl.pallas_call(functools.partial(kernel, n_y, n_z), name='section', out_s...  57 us
    unnamed x4, local copies, waits for them, and re-layouts  3.34 us

profile of v1, /device:TPU:23, one launch (start us, length us, event | category | flops | bytes accessed | tf_op | source)
XLA Modules:
  0.0 65.5 jit_solution(5696016762767744548)
XLA Ops:
  1.3 1.3 %reshape.13.own_ref = s32[1,1152]{1,0:T(1,128)} reshape(s32[1152]{0:T(1024)} %param.10) | data formatting | bytes 9216 | tf_op jit(solution)/shard_map/reshape | solution.py:673
  2.6 1.3 %reshape.14.chord_ref = f32[1,1152]{1,0:T(1,128)} reshape(f32[1152]{0:T(1024)} %param.13) | data formatting | bytes 9216 | tf_op jit(solution)/shard_map/reshape | solution.py:674
  3.9 1.3 %reshape.15.twist_ref = f32[1,1152]{1,0:T(1,128)} reshape(f32[1152]{0:T(1024)} %param.14) | data formatting | bytes 9216 | tf_op jit(solution)/shard_map/reshape | solution.py:674
  5.2 57.0 %section.1 = (f32[3,16,64,128]{3,2,1,0:T(8,128)}, f32[3,1152]{1,0:T(4,128)}) custom-call(f32[3,16,64,128]{3,2,1,0:T(8,128)} %om_hbm.1, f32[3,16,64,128]{3,2,1,0:T(8,128)} %ve_hbm.1, s32[1,1152]{1,0:T(1,128)} %reshape.13.own_ref, s32[3,1152]{1,0:T(4,128)} %cell_ref.1, f32[3,1152]{1,0:T(4,128)} %frac_ref.1, f32[1,1152]{1,0:T(1,128)} %reshape.14.chord_ref, ...), custom_call_target="tpu_custom_call" | custom-call | tf_op jit(solution)/shard_map/section/pallas_call | solution.py:661
  62.2 0.0 copy-start
  62.2 2.7 %copy.13 = f32[3,16,64,128]{3,2,1,0:T(8,128)} copy(f32[3,16,64,128]{3,2,1,0:T(8,128)} %get-tuple-element.4) | data formatting | bytes 3145728
  64.9 0.0 copy-done
  64.9 0.6 copy.14
Async XLA Ops:
  62.2 2.7 %copy-start = (f32[3,1152]{1,0:T(4,128)S(1)}, f32[3,1152]{1,0:T(4,128)}, u32[]{:S(2)}) copy-start(f32[3,1152]{1,0:T(4,128)} %get-tuple-element.5) | copy-start | bytes 41476

commit v2 on v1

--- a/solution.py
+++ b/solution.py
@@ -66,10 +66,10 @@
 def kernel(
     n_y, n_z,
     om_hbm, ve_hbm, own_ref, cell_ref, frac_ref, chord_ref, twist_ref, ang_ref,
-    out_hbm, src_out,
-    vb, wb, sb, mb, yb, wx, wy, wz, zs, zr, ks, kr, ob,
-    vals, sel, pk, p1r, p2s, p2r, p3s, p3r, pvb, srcb, ab,
-    ld_sem, ys, yr, zss, zsr, p1s, p1v, p2ss, p2v, p3ss, p3v, ms, mr, kss, ksr, osem,
+    out_ref, src_out,
+    vb, wb, sb, mb, yb, wx, wy, wz, zs, zr, ks, kr,
+    vals, sel, pk, p1r, p2s, p2r, p3s, p3r, pvb, tall, ab,
+    ld_sem, ys, yr, zss, zsr, p1s, p1v, p2ss, p2v, p3ss, p3v, ms, mr, kss, ksr,
 ):
     gy = lax.axis_index("gy")
     gz = lax.axis_index("gz")
@@ -87,19 +87,30 @@
     has_l, has_r = gz > 0, gz < n_z - 1
     in_span = gy < NS
     is_src = in_span & (gz >= vb0) & (gz < vb0 + nvb)
+    place = gy % span
+
+    def peer(d):
+        return t_own * span + lax.rem(place + d, span)
+
 
     bar = pltpu.get_barrier_semaphore()
     for d in range(1, n_z):
         pl.semaphore_signal(bar, inc=1, device_id=(gy, lax.rem(gz + d, n_z)), device_id_type=MESH)
-    for d in range(1, 8):
-        pl.semaphore_signal(
-            bar, inc=1, device_id=(zc * 8 + lax.rem(plane + d, 8), gz), device_id_type=MESH)
     for d in range(1, n_zc):
         pl.semaphore_signal(
             bar, inc=1, device_id=(lax.rem(zc + d, n_zc) * 8 + plane, gz), device_id_type=MESH)
-    n_bar = (n_z - 1) + 7 + (n_zc - 1)
-    cross_dn = has_dn & (plane == 0)
-    cross_up = has_up & (plane == 7)
+
+    @pl.when(in_span)
+    def _():
+        for d in range(1, span):
+            pl.semaphore_signal(bar, inc=1, device_id=(peer(d), gz), device_id_type=MESH)
+
+    loose = jnp.logical_not(in_span)
+    cross_dn = has_dn & ((place == 0) | loose)
+    cross_up = has_up & ((place == span - 1) | loose)
+    n_bar = (
+        (n_z - 1) + (n_zc - 1) + jnp.where(in_span, span - 1, 0)
+        + cross_dn.astype(jnp.int32) + cross_up.astype(jnp.int32))
 
     @pl.when(cross_dn)
     def _():
@@ -146,13 +157,6 @@
     @pl.when(jnp.logical_not(has_up))
     def _():
         zero_y(CY + 2)
-
-    @pl.when((zc + 1) * 8 > NS)
-    def _():
-        for s in range(8):
-            @pl.when(zc * 8 + s >= NS)
-            def _():
-                p2r[s] = ztile
 
     vals[0:3, :] = cell_ref[...].astype(F32)
     vals[3:6, :] = frac_ref[...]
@@ -163,8 +167,8 @@
     sb128 = lax.broadcasted_iota(jnp.int32, (128, 128), 0)
     base0 = pl.multiple_of(rb * 128, 128)
     base1 = pl.multiple_of(rb * 128 + 128, 128)
-    o0 = jnp.broadcast_to(own_ref[:, pl.ds(base0, 128)], (8, 128))
-    o1 = jnp.broadcast_to(own_ref[:, pl.ds(base1, 128)], (8, 128))
+    o0 = jnp.broadcast_to(own_ref[pl.ds(base0, 128)].reshape(1, 128), (8, 128))
+    o1 = jnp.broadcast_to(own_ref[pl.ds(base1, 128)].reshape(1, 128), (8, 128))
     own = jnp.where(row8 == 0, o0, jnp.where(row8 == 1, o1, -1))
     mine = own == my_block
     mf = mine.astype(F32)
@@ -206,35 +210,6 @@
 
     lax.fori_loop(0, 12, pack, 0)
 
-    pl.semaphore_wait(bar, n_bar + cross_dn.astype(jnp.int32) + cross_up.astype(jnp.int32))
-
-    def rcopy(src, dst, ss, rs, dev):
-        return pltpu.make_async_remote_copy(
-            src_ref=src, dst_ref=dst, send_sem=ss, recv_sem=rs, device_id=dev, device_id_type=MESH)
-
-    def z_copy(d):
-        return rcopy(zs.at[d], zr.at[d], zss.at[d], zsr.at[d], (gy, gz + (1 if d == 0 else -1)))
-
-    def y_copy(f, d):
-        buf = vb if f == 0 else wb
-        src, dst = (CY, 0) if d == 0 else (2, CY + 2)
-        return rcopy(
-            buf.at[:, pl.ds(src, 2), pl.ds(8, CZ)], buf.at[:, pl.ds(dst, 2), pl.ds(8, CZ)],
-            ys.at[f, d], yr.at[f, d], (gy + (1 if d == 0 else -1), gz))
-
-    up_cond = ((has_up, has_dn), (has_dn, has_up))
-    rt_cond = ((has_r, has_l), (has_l, has_r))
-    for d in range(2):
-        @pl.when(rt_cond[d][0])
-        def _():
-            z_copy(d).start()
-
-    for f in range(2):
-        for d in range(2):
-            @pl.when(up_cond[d][0])
-            def _():
-                y_copy(f, d).start()
-
     def sample(y, acc):
         wyr = tyq_row(y)
         out = []
@@ -262,6 +237,53 @@
     packet = lax.dot_general(qa, s0, dnt, precision=HI, preferred_element_type=F32)
     packet = packet + lax.dot_general(qb, s1, dnt, precision=HI, preferred_element_type=F32)
 
+    def trig(rows, twist):
+        col = lax.broadcasted_iota(jnp.int32, rows.shape, 1)
+        station = col % BP
+        blade = (2 * rows + col // BP) % BLADES
+        theta = ang_ref[0].astype(F32) * turn_step
+        theta = theta + 2.0 * 3.141592653589793 / 3.0 * blade.astype(F32)
+        radius = (station.astype(F32) + 0.5) / BP
+        return station, tip_speed * radius, jnp.cos(theta), jnp.sin(theta), jnp.cos(twist), jnp.sin(twist)
+
+    def forces(angles, chord, pv):
+        station, reach, cos_t, sin_t, cos_w, sin_w = angles
+        rel_x = pv[0]
+        rel_y = pv[1] + reach * sin_t
+        rel_z = pv[2] - reach * cos_t
+        rel_t = -sin_t * rel_y + cos_t * rel_z
+        speed = jnp.sqrt(rel_x * rel_x + rel_t * rel_t + 1.0)
+        gamma = 3.141592653589793 * chord * (rel_x * cos_w + rel_t * sin_w)
+        before = jnp.where(station == 0, 0.0, pltpu.roll(gamma, 1, 1))
+        ratio = (gamma - before) / speed
+        return [ratio * rel_x, gamma * cos_t + ratio * rel_y, gamma * sin_t + ratio * rel_z]
+
+    def pick(a, b):
+        a, b = jnp.broadcast_to(a, (8, 128)), jnp.broadcast_to(b, (8, 128))
+        return jnp.where(row8 == 0, a, jnp.where(row8 == 1, b, 0.0))
+
+    def pair(ref):
+        return pick(ref[pl.ds(base0, 128)].reshape(1, 128), ref[pl.ds(base1, 128)].reshape(1, 128))
+
+    trig2 = trig(row8 + rb, pair(twist_ref))
+    chord2 = pair(chord_ref)
+
+    pl.semaphore_wait(bar, n_bar)
+
+    def rcopy(src, dst, ss, rs, dev):
+        return pltpu.make_async_remote_copy(
+            src_ref=src, dst_ref=dst, send_sem=ss, recv_sem=rs, device_id=dev, device_id_type=MESH)
+
+    def z_copy(d):
+        return rcopy(zs.at[d], zr.at[d], zss.at[d], zsr.at[d], (gy, gz + (1 if d == 0 else -1)))
+
+    def y_copy(f, d):
+        buf = vb if f == 0 else wb
+        src, dst = (CY, 0) if d == 0 else (2, CY + 2)
+        return rcopy(
+            buf.at[:, pl.ds(src, 2), pl.ds(8, CZ)], buf.at[:, pl.ds(dst, 2), pl.ds(8, CZ)],
+            ys.at[f, d], yr.at[f, d], (gy + (1 if d == 0 else -1), gz))
+
     def p1_copy(d):
         return rcopy(pk, p1r.at[gz - vb0], p1s.at[d - 1], p1v.at[gz - vb0],
                      (gy, lax.rem(gz + d, n_z)))
@@ -272,6 +294,19 @@
         p1r[gz - vb0] = packet
         for d in range(1, n_z):
             p1_copy(d).start()
+
+    up_cond = ((has_up, has_dn), (has_dn, has_up))
+    rt_cond = ((has_r, has_l), (has_l, has_r))
+    for d in range(2):
+        @pl.when(rt_cond[d][0])
+        def _():
+            z_copy(d).start()
+
+    for f in range(2):
+        for d in range(2):
+            @pl.when(up_cond[d][0])
+            def _():
+                y_copy(f, d).start()
 
     lanes = lax.broadcasted_iota(jnp.int32, (CHUNK, NX), 1)
 
@@ -303,16 +338,19 @@
         for s in range(1, nvb):
             tile = tile + p1r[s]
         p2s[...] = tile
-        p2r[plane] = tile
+        p2r[0] = tile
 
     def p2_copy(d):
-        return rcopy(p2s, p2r.at[plane], p2ss.at[d - 1], p2v.at[plane],
-                     (zc * 8 + lax.rem(plane + d, 8), gz))
+        return rcopy(p2s, p2r.at[d], p2ss.at[d - 1], p2v.at[d], (peer(d), gz))
 
     @pl.when(in_span)
     def _():
-        for d in range(1, 8):
+        for d in range(1, span):
             p2_copy(d).start()
+
+    def p3_copy(d):
+        return rcopy(p3s, p3r.at[zc], p3ss.at[d - 1], p3v.at[zc],
+                     (lax.rem(zc + d, n_zc) * 8 + plane, gz))
 
     def wz_loop(y, carry):
         for z0 in range(0, CZ, CHUNK):
@@ -334,31 +372,6 @@
         return carry
 
     lax.fori_loop(0, CY, wy_loop, 0)
-
-    for s in range(8):
-        @pl.when((plane != s) & (zc * 8 + s < NS))
-        def _():
-            rcopy(p2r.at[s], p2r.at[s], p2ss.at[0], p2v.at[s], (gy, gz)).wait_recv()
-
-    t_a = (zc * 8) // span
-    suma = jnp.zeros((8, 128), F32)
-    sumb = suma
-    for s in range(8):
-        x = p2r[s]
-        first = (zc * 8 + s) // span == t_a
-        suma = suma + jnp.where(first, x, 0.0)
-        sumb = sumb + jnp.where(first, 0.0, x)
-    p3s[0] = suma
-    p3s[1] = sumb
-    p3r[zc, 0] = suma
-    p3r[zc, 1] = sumb
-
-    def p3_copy(d):
-        return rcopy(p3s, p3r.at[zc], p3ss.at[d - 1], p3v.at[zc],
-                     (lax.rem(zc + d, n_zc) * 8 + plane, gz))
-
-    for d in range(1, n_zc):
-        p3_copy(d).start()
 
     for d in range(2):
         @pl.when(rt_cond[d][1])
@@ -432,71 +445,52 @@
 
     lax.fori_loop(0, CY, section_loop, 0)
 
-    for s in range(n_zc):
-        @pl.when(zc != s)
-        def _():
-            rcopy(p3r.at[s], p3r.at[s], p3ss.at[0], p3v.at[s], (gy, gz)).wait_recv()
-
-    tiles = [jnp.zeros((8, 128), F32) for _ in range(TURBINES)]
-    for s in range(n_zc):
-        ta = (s * 8) // span
-        if ta < TURBINES:
-            tiles[ta] = tiles[ta] + p3r[s, 0]
-        if ta + 1 < TURBINES:
-            tiles[ta + 1] = tiles[ta + 1] + p3r[s, 1]
-    for u in range(TURBINES // 2):
-        e, o = tiles[2 * u], tiles[2 * u + 1]
-        for c in range(3):
-            pvb[c, 3 * u:3 * u + 1, :] = e[c:c + 1]
-            pvb[c, 3 * u + 1:3 * u + 2, :] = e[4 + c:5 + c] + o[c:c + 1]
-            pvb[c, 3 * u + 2:3 * u + 3, :] = o[4 + c:5 + c]
-    n_rows = TURBINES * BLADES * BP // 128
-    for r in range(n_rows):
-        pvb[3, r:r + 1, :] = chord_ref[:, 128 * r:128 * r + 128]
-        pvb[4, r:r + 1, :] = twist_ref[:, 128 * r:128 * r + 128]
-    r16 = lax.broadcasted_iota(jnp.int32, (16, 128), 0)
-    l16 = lax.broadcasted_iota(jnp.int32, (16, 128), 1)
-    live = r16 < n_rows
-    station = l16 % BP
-    blade = (2 * r16 + l16 // BP) % BLADES
-    theta = ang_ref[0].astype(F32) * turn_step + 2.0 * 3.141592653589793 / 3.0 * blade.astype(F32)
-    radius = (station.astype(F32) + 0.5) / BP
-    cos_t = jnp.cos(theta)
-    sin_t = jnp.sin(theta)
-    chord = jnp.where(live, pvb[3], 0.0)
-    twist = jnp.where(live, pvb[4], 0.0)
-    rel_x = jnp.where(live, pvb[0], 0.0)
-    rel_y = jnp.where(live, pvb[1], 0.0) + tip_speed * radius * sin_t
-    rel_z = jnp.where(live, pvb[2], 0.0) - tip_speed * radius * cos_t
-    rel_t = -sin_t * rel_y + cos_t * rel_z
-    speed = jnp.sqrt(rel_x * rel_x + rel_t * rel_t + 1.0)
-    gamma = 3.141592653589793 * chord * (rel_x * jnp.cos(twist) + rel_t * jnp.sin(twist))
-    before = jnp.where(station == 0, 0.0, pltpu.roll(gamma, 1, 1))
-    ratio = (gamma - before) / speed
-    src = [ratio * rel_x, gamma * cos_t + ratio * rel_y, gamma * sin_t + ratio * rel_z]
-    for r in range(n_rows):
-        srcb[r, 3:8, :] = jnp.zeros((5, 128), F32)
-        for c in range(3):
-            src_out[c:c + 1, 128 * r:128 * r + 128] = src[c][r:r + 1]
-            srcb[r, c:c + 1, :] = src[c][r:r + 1]
-    srcq = jnp.dot(srcb[rb], sel[0], precision=HI, preferred_element_type=F32)
-    srcq = srcq + jnp.dot(srcb[rb + 1], sel[1], precision=HI, preferred_element_type=F32)
-    tyq2 = ab[0]
-    for c in range(3):
-        ab[c + 1] = section_step * tyq2 * srcq[c:c + 1, :]
+    @pl.when(in_span)
+    def _():
+        for d in range(1, span):
+            rcopy(p2r.at[d], p2r.at[d], p2ss.at[0], p2v.at[d], (gy, gz)).wait_recv()
+        tile = p2r[0]
+        for d in range(1, span):
+            tile = tile + p2r[d]
+        p3s[...] = tile
+        p3r[zc] = tile
+        for d in range(1, n_zc):
+            p3_copy(d).start()
+
+    @pl.when(is_src)
+    def _():
+        tile = p3s[...]
+        pv2 = [pick(tile[c:c + 1], tile[4 + c:5 + c]) for c in range(3)]
+        src = forces(trig2, chord2, pv2)
+        e0 = jnp.zeros((8, 128), F32)
+        e1 = e0
+        for c in range(3):
+            e0 = jnp.where(row8 == c, jnp.broadcast_to(src[c][0:1], (8, 128)), e0)
+            e1 = jnp.where(row8 == c, jnp.broadcast_to(src[c][1:2], (8, 128)), e1)
+        srcq = jnp.dot(e0, sel[0], precision=HI, preferred_element_type=F32)
+        srcq = srcq + jnp.dot(e1, sel[1], precision=HI, preferred_element_type=F32)
+        for c in range(3):
+            ab[c + 1] = section_step * ab[0] * srcq[c:c + 1, :]
 
     def move_x(y):
         for c in range(3):
-            lhs = split(tzq * ab[c + 1, pl.ds(y, 1), :])
-            smear = dot3(lhs, txs, ((1,), (1,)))
-            f_all = sb[c, y] + smear
             for z0 in range(0, CZ, CHUNK):
-                f = f_all[z0:z0 + CHUNK]
+                f = sb[c, y, pl.ds(z0, CHUNK), :]
                 g = wx[2, y, pl.ds(z0, CHUNK), :] * f
                 for k in (0, 1, 3, 4):
                     p = wx[k, y, pl.ds(z0, CHUNK), :] * f
                     g = g + pltpu.roll(p, (k - 2) % NX, 1)
                 mb[c, y + 2, pl.ds(z0, CHUNK), :] = g
+
+    def smear_loop(y, carry):
+        for c in range(3):
+            lhs = split(tzq * ab[c + 1, pl.ds(y, 1), :])
+            sb[c, y] = sb[c, y] + dot3(lhs, txs, ((1,), (1,)))
+        return carry
+
+    @pl.when(is_src)
+    def _():
+        lax.fori_loop(0, CY, smear_loop, 0)
 
     def edge_loop(i, carry):
         move_x(jnp.where(i < 2, i, i + CY - 4))
@@ -585,12 +579,39 @@
                 g = w[0] * yb[c, y, pl.ds(8 + z0 + 2, CHUNK), :]
                 for k in range(1, 5):
                     g = g + w[k] * yb[c, y, pl.ds(8 + z0 + 2 - k, CHUNK), :]
-                ob[c, y, pl.ds(z0, CHUNK), :] = g
+                out_ref[c, y, pl.ds(z0, CHUNK), :] = g
         return carry
 
     lax.fori_loop(0, CY, move_z, 0)
-    oc = pltpu.make_async_copy(ob, out_hbm, osem)
-    oc.start()
+
+    for s in range(n_zc):
+        @pl.when((zc != s) & (s * 8 + plane < NS))
+        def _():
+            rcopy(p3r.at[s], p3r.at[s], p3ss.at[0], p3v.at[s], (gy, gz)).wait_recv()
+
+    for s in range(n_zc):
+        @pl.when(s * 8 + plane < NS)
+        def _():
+            tall[(s * 8 + plane) // span] = p3r[s]
+
+    for u in range(TURBINES // 2):
+        e, o = tall[2 * u], tall[2 * u + 1]
+        for c in range(3):
+            pvb[c, 3 * u:3 * u + 1, :] = e[c:c + 1]
+            pvb[c, 3 * u + 1:3 * u + 2, :] = e[4 + c:5 + c] + o[c:c + 1]
+            pvb[c, 3 * u + 2:3 * u + 3, :] = o[4 + c:5 + c]
+    n_rows = TURBINES * BLADES * BP // 128
+    for r in range(n_rows):
+        pvb[3, r:r + 1, :] = chord_ref[128 * r:128 * r + 128].reshape(1, 128)
+        pvb[4, r:r + 1, :] = twist_ref[128 * r:128 * r + 128].reshape(1, 128)
+    r16 = lax.broadcasted_iota(jnp.int32, (16, 128), 0)
+    live = r16 < n_rows
+    full = forces(
+        trig(r16, jnp.where(live, pvb[4], 0.0)), jnp.where(live, pvb[3], 0.0),
+        [jnp.where(live, pvb[c], 0.0) for c in range(3)])
+    for r in range(n_rows):
+        for c in range(3):
+            src_out[c:c + 1, 128 * r:128 * r + 128] = full[c][r:r + 1]
 
     for d in range(2):
         @pl.when(rt_cond[d][0])
@@ -611,12 +632,10 @@
 
     @pl.when(in_span)
     def _():
-        for d in range(1, 8):
+        for d in range(1, span):
             p2_copy(d).wait_send()
-
-    for d in range(1, n_zc):
-        p3_copy(d).wait_send()
-    oc.wait()
+        for d in range(1, n_zc):
+            p3_copy(d).wait_send()
 
 
 def on_device(n_y, n_z, omega, velocity, owner, cells, frac, chord, twist, angle):
@@ -642,36 +661,34 @@
         V((2, 2, 3, cy // 4, 8, nx), F32),
         V((2, 3, cy // 4, 8, nx), F32),
         V((2, 3, cy // 4, 8, nx), F32),
-        V((3, cy, cz, nx), F32),
         V((8, n_p), F32),
         V((2, 128, 128), F32),
         V((8, 128), F32),
         V((nvb, 8, 128), F32),
         V((8, 128), F32),
-        V((8, 8, 128), F32),
-        V((2, 8, 128), F32),
-        V((n_zc, 2, 8, 128), F32),
+        V((n_y // TURBINES, 8, 128), F32),
+        V((8, 128), F32),
+        V((n_zc, 8, 128), F32),
         V((5, 16, 128), F32),
-        V((n_p // 128, 8, 128), F32),
+        V((TURBINES, 8, 128), F32),
         V((4, cy, 128), F32),
         D((6,)), D((2, 2)), D((2, 2)), D((2,)), D((2,)),
-        D((n_z - 1,)), D((nvb,)), D((7,)), D((8,)), D((n_zc - 1,)), D((n_zc,)),
-        D((2,)), D((2,)), D((2,)), D((2,)), D(()),
+        D((n_z - 1,)), D((nvb,)), D((n_y // TURBINES - 1,)), D((n_y // TURBINES,)), D((n_zc - 1,)), D((n_zc,)),
+        D((2,)), D((2,)), D((2,)), D((2,)),
     ]
     out, src = pl.pallas_call(
         functools.partial(kernel, n_y, n_z),
         name="section",
         out_shape=(
-            jax.ShapeDtypeStruct(omega.shape, F32),
+            pltpu.VMEM(omega.shape, F32),
             jax.ShapeDtypeStruct((3, n_p), F32),
         ),
         in_specs=[hb, hb, vm, vm, vm, vm, vm, sm],
-        out_specs=(hb, vm),
+        out_specs=(vm, vm),
         scratch_shapes=scratch,
         compiler_params=pltpu.CompilerParams(
             collective_id=0, has_side_effects=True, vmem_limit_bytes=60 * 1024 * 1024),
-    )(omega, velocity, owner.reshape(1, n_p), cells, frac,
-      chord.reshape(1, n_p), twist.reshape(1, n_p), angle)
+    )(omega, velocity, owner, cells, frac, chord, twist, angle)
     return out, src
 
 

time: 65.9 us -> 54.3 us (0.82)
  the two profiles are of different devices: /device:TPU:23 before, /device:TPU:262 now
where the time goes in v2:
time: 54.3 us; the launch traced here: 54.1 us
  Pallas kernels  51 us (94%)
  local copies, waits for them, and re-layouts  1.76 us (3%)
  between operations  1.3 us (2%)
    pallas_call x1, Pallas kernels, on_device(): pl.pallas_call(functools.partial(kernel, n_y, n_z), name='section', out_s...  51 us
    unnamed x4, local copies, waits for them, and re-layouts  1.76 us

profile of v2, /device:TPU:262, one launch (start us, length us, event | category | flops | bytes accessed | tf_op | source)
XLA Modules:
  0.0 54.1 jit_solution(15770855806873823093)
XLA Ops:
  1.3 51.0 %section.1 = (f32[3,16,64,128]{3,2,1,0:T(8,128)S(1)}, f32[3,1152]{1,0:T(4,128)}) custom-call(f32[3,16,64,128]{3,2,1,0:T(8,128)} %om_hbm.1, f32[3,16,64,128]{3,2,1,0:T(8,128)} %ve_hbm.1, s32[1152]{0:T(1024)} %own_ref.1, s32[3,1152]{1,0:T(4,128)} %cell_ref.1, f32[3,1152]{1,0:T(4,128)} %frac_ref.1, f32[1152]{0:T(1024)} %chord_ref.1, f32[1152]{0:T(1024)} %twist_ref.1, ...), custom_call_target="tpu_custom_call" | custom-call | tf_op jit(solution)/shard_map/section/pallas_call | solution.py:679
  52.3 0.0 copy-start
  52.3 1.1 %copy.12 = f32[3,16,64,128]{3,2,1,0:T(8,128)} copy(f32[3,16,64,128]{3,2,1,0:T(8,128)S(1)} %get-tuple-element.2) | data formatting | bytes 3145728
  53.5 0.0 copy-done
  53.5 0.6 %copy.14 = f32[3,1152]{1,0:T(4,128)} copy(f32[3,1152]{1,0:T(4,128)S(1)} %copy-done) | data formatting | bytes 27648
Async XLA Ops:
  52.3 1.2 %copy-start = (f32[3,1152]{1,0:T(4,128)S(1)}, f32[3,1152]{1,0:T(4,128)}, u32[]{:S(2)}) copy-start(f32[3,1152]{1,0:T(4,128)} %get-tuple-element.7) | copy-start | bytes 41476

commit v3 on v2

--- a/solution.py
+++ b/solution.py
@@ -68,7 +68,7 @@
     om_hbm, ve_hbm, own_ref, cell_ref, frac_ref, chord_ref, twist_ref, ang_ref,
     out_ref, src_out,
     vb, wb, sb, mb, yb, wx, wy, wz, zs, zr, ks, kr,
-    vals, sel, pk, p1r, p2s, p2r, p3s, p3r, pvb, tall, ab,
+    vals, sel, pk, p1r, p2s, p2r, p3s, p3r, pvb, tall, ab, txb, tzb,
     ld_sem, ys, yr, zss, zsr, p1s, p1v, p2ss, p2v, p3ss, p3v, ms, mr, kss, ksr,
 ):
     gy = lax.axis_index("gy")
@@ -194,6 +194,9 @@
     tyq = table(CY, 1)
     tzq = table(CZ, 2)
     txs = split(tx)
+    txb[0] = txs[0]
+    txb[1] = txs[1]
+    tzb[...] = tzq
 
     for cp in loads:
         cp.wait()
@@ -215,7 +218,7 @@
         out = []
         for c in range(3):
             v = split(vb[c, y + 2, pl.ds(8, CZ), :])
-            col = dot3(v, txs, ((1,), (0,))) * tzq
+            col = dot3(v, (txb[0], txb[1]), ((1,), (0,))) * tzb[...]
             s = jnp.sum(col, axis=0, keepdims=True)
             out.append(acc[c] + s * wyr)
         return tuple(out)
@@ -277,12 +280,15 @@
     def z_copy(d):
         return rcopy(zs.at[d], zr.at[d], zss.at[d], zsr.at[d], (gy, gz + (1 if d == 0 else -1)))
 
-    def y_copy(f, d):
+    PARTS = ((0, 8), (CZ - 8, 8), (8, CZ - 16))
+
+    def y_copy(f, d, part):
         buf = vb if f == 0 else wb
         src, dst = (CY, 0) if d == 0 else (2, CY + 2)
+        z0, n = PARTS[part]
         return rcopy(
-            buf.at[:, pl.ds(src, 2), pl.ds(8, CZ)], buf.at[:, pl.ds(dst, 2), pl.ds(8, CZ)],
-            ys.at[f, d], yr.at[f, d], (gy + (1 if d == 0 else -1), gz))
+            buf.at[:, pl.ds(src, 2), pl.ds(8 + z0, n)], buf.at[:, pl.ds(dst, 2), pl.ds(8 + z0, n)],
+            ys.at[f, d, part], yr.at[f, d, part], (gy + (1 if d == 0 else -1), gz))
 
     def p1_copy(d):
         return rcopy(pk, p1r.at[gz - vb0], p1s.at[d - 1], p1v.at[gz - vb0],
@@ -302,15 +308,16 @@
         def _():
             z_copy(d).start()
 
-    for f in range(2):
+    for parts in ((0, 1), (2,)):
         for d in range(2):
             @pl.when(up_cond[d][0])
             def _():
-                y_copy(f, d).start()
-
-    lanes = lax.broadcasted_iota(jnp.int32, (CHUNK, NX), 1)
+                for f in range(2):
+                    for part in parts:
+                        y_copy(f, d, part).start()
 
     def wx_loop(y, carry):
+        lanes = lax.broadcasted_iota(jnp.int32, (CHUNK, NX), 1)
         for z0 in range(0, CZ, CHUNK):
             w = remesh_weights(vb[0, y + 2, pl.ds(8 + z0, CHUNK), :])
             for k in range(5):
@@ -323,10 +330,88 @@
                 wx[k, y, pl.ds(z0, CHUNK), :] = x
         return carry
 
+    def wz_loop(y, carry):
+        for z0 in range(0, CZ, CHUNK):
+            w = remesh_weights(vb[2, y + 2, pl.ds(8 + z0, CHUNK), :])
+            for k in range(5):
+                wz[k, y, pl.ds(8 + z0, CHUNK), :] = w[k]
+        return carry
+
+    def wz_edge(y, carry):
+        for r0 in (0, 8 + CZ):
+            w = remesh_weights(vb[2, y + 2, pl.ds(r0, 8), :])
+            for k in range(5):
+                wz[k, y, pl.ds(r0, 8), :] = w[k]
+        return carry
+
+    def wy_one(y, rows):
+        for z0, n in rows:
+            w = remesh_weights(vb[1, y, pl.ds(8 + z0, n), :])
+            for k in range(5):
+                wy[k, y, pl.ds(z0, n), :] = w[k]
+
+    def wy_loop(y, carry):
+        wy_one(y + 2, ((0, CHUNK), (CHUNK, CHUNK)))
+        return carry
+
+    c0 = section_step / 12.0
+    cl = section_step * viscosity / 12.0
+
+    def around(buf, c, y, z0, n, dim):
+        if dim == 2:
+            return [buf[c, y + 2 + k, pl.ds(8 + z0, n), :] for k in (-2, -1, 1, 2)]
+        if dim == 1:
+            return [buf[c, y + 2, pl.ds(8 + z0 + k, n), :] for k in (-2, -1, 1, 2)]
+        f = buf[c, y + 2, pl.ds(8 + z0, n), :]
+        lanes = lax.broadcasted_iota(jnp.int32, (n, NX), 1)
+        res = []
+        for k in (-2, -1, 1, 2):
+            r = pltpu.roll(f, (-k) % NX, 1)
+            m = lanes >= -k if k < 0 else lanes < NX - k
+            res.append(jnp.where(m, r, 0.0))
+        return res
+
+    def section_rows(y, rows):
+        for z0, n in rows:
+            om = [wb[c, y + 2, pl.ds(8 + z0, n), :] for c in range(3)]
+            oms = [c0 * o for o in om]
+            for c in range(3):
+                acc = om[c]
+                near = None
+                far = None
+                for dim in range(3):
+                    a = around(vb, c, y, z0, n, dim)
+                    acc = acc + oms[2 - dim] * (8.0 * (a[2] - a[1]) - (a[3] - a[0]))
+                    b = around(wb, c, y, z0, n, dim)
+                    p = b[1] + b[2]
+                    e = b[0] + b[3]
+                    near = p if near is None else near + p
+                    far = e if far is None else far + e
+                acc = acc + cl * (16.0 * near - far - 90.0 * om[c])
+                sb[c, y, pl.ds(z0, n), :] = acc
+
+    RIM = ((0, 8), (CZ - 8, 8))
+    half = (CZ - 16) // 2
+    MID = ((8, half), (8 + half, half))
+
+    def edge_y(i):
+        return jnp.where(i < 2, i, i + CY - 4)
+
+    def run(n, fn):
+        def step(i, carry):
+            fn(i)
+            return carry
+
+        lax.fori_loop(0, n, step, 0)
+
     lax.fori_loop(0, CY, wx_loop, 0)
+    run(CY - 4, lambda i: section_rows(i + 2, MID))
 
     def p1_wait(s):
         return rcopy(p1r.at[s], p1r.at[s], p1s.at[0], p1v.at[s], (gy, gz))
+
+    def p2_copy(d):
+        return rcopy(p2s, p2r.at[d], p2ss.at[d - 1], p2v.at[d], (peer(d), gz))
 
     @pl.when(in_span)
     def _():
@@ -339,38 +424,10 @@
             tile = tile + p1r[s]
         p2s[...] = tile
         p2r[0] = tile
-
-    def p2_copy(d):
-        return rcopy(p2s, p2r.at[d], p2ss.at[d - 1], p2v.at[d], (peer(d), gz))
-
-    @pl.when(in_span)
-    def _():
         for d in range(1, span):
             p2_copy(d).start()
 
-    def p3_copy(d):
-        return rcopy(p3s, p3r.at[zc], p3ss.at[d - 1], p3v.at[zc],
-                     (lax.rem(zc + d, n_zc) * 8 + plane, gz))
-
-    def wz_loop(y, carry):
-        for z0 in range(0, CZ, CHUNK):
-            w = remesh_weights(vb[2, y + 2, pl.ds(8 + z0, CHUNK), :])
-            for k in range(5):
-                wz[k, y, pl.ds(8 + z0, CHUNK), :] = w[k]
-        return carry
-
     lax.fori_loop(0, CY, wz_loop, 0)
-
-    def wy_one(y):
-        for z0 in range(0, CZ, CHUNK):
-            w = remesh_weights(vb[1, y, pl.ds(8 + z0, CHUNK), :])
-            for k in range(5):
-                wy[k, y, pl.ds(z0, CHUNK), :] = w[k]
-
-    def wy_loop(y, carry):
-        wy_one(y + 2)
-        return carry
-
     lax.fori_loop(0, CY, wy_loop, 0)
 
     for d in range(2):
@@ -389,61 +446,23 @@
 
             lax.fori_loop(0, 12, unpack, 0)
 
-    def wz_edge(y, carry):
-        for r0 in (0, 8 + CZ):
-            w = remesh_weights(vb[2, y + 2, pl.ds(r0, 8), :])
-            for k in range(5):
-                wz[k, y, pl.ds(r0, 8), :] = w[k]
-        return carry
-
     lax.fori_loop(0, CY, wz_edge, 0)
+    run(CY - 4, lambda i: section_rows(i + 2, RIM))
 
     for f in range(2):
         for d in range(2):
             @pl.when(up_cond[d][1])
             def _():
-                y_copy(f, d).wait_recv()
-
+                for part in range(2):
+                    y_copy(f, d, part).wait_recv()
+
+    run(4, lambda i: section_rows(edge_y(i), RIM))
     for y in (0, 1, CY + 2, CY + 3):
-        wy_one(y)
-
-    c0 = section_step / 12.0
-    cl = section_step * viscosity / 12.0
-
-    def around(buf, c, y, z0, dim):
-        if dim == 2:
-            return [buf[c, y + 2 + k, pl.ds(8 + z0, CHUNK), :] for k in (-2, -1, 1, 2)]
-        if dim == 1:
-            return [buf[c, y + 2, pl.ds(8 + z0 + k, CHUNK), :] for k in (-2, -1, 1, 2)]
-        f = buf[c, y + 2, pl.ds(8 + z0, CHUNK), :]
-        res = []
-        for k in (-2, -1, 1, 2):
-            r = pltpu.roll(f, (-k) % NX, 1)
-            m = lanes >= -k if k < 0 else lanes < NX - k
-            res.append(jnp.where(m, r, 0.0))
-        return res
-
-    def section_loop(y, carry):
-        for z0 in range(0, CZ, CHUNK):
-            om = [wb[c, y + 2, pl.ds(8 + z0, CHUNK), :] for c in range(3)]
-            oms = [c0 * o for o in om]
-            for c in range(3):
-                acc = om[c]
-                near = None
-                far = None
-                for dim in range(3):
-                    a = around(vb, c, y, z0, dim)
-                    acc = acc + oms[2 - dim] * (8.0 * (a[2] - a[1]) - (a[3] - a[0]))
-                    b = around(wb, c, y, z0, dim)
-                    n = b[1] + b[2]
-                    e = b[0] + b[3]
-                    near = n if near is None else near + n
-                    far = e if far is None else far + e
-                acc = acc + cl * (16.0 * near - far - 90.0 * om[c])
-                sb[c, y, pl.ds(z0, CHUNK), :] = acc
-        return carry
-
-    lax.fori_loop(0, CY, section_loop, 0)
+        wy_one(y, RIM)
+
+    def p3_copy(d):
+        return rcopy(p3s, p3r.at[zc], p3ss.at[d - 1], p3v.at[zc],
+                     (lax.rem(zc + d, n_zc) * 8 + plane, gz))
 
     @pl.when(in_span)
     def _():
@@ -454,8 +473,19 @@
             tile = tile + p2r[d]
         p3s[...] = tile
         p3r[zc] = tile
-        for d in range(1, n_zc):
-            p3_copy(d).start()
+
+    def smear_rows(y, spans):
+        lhs = []
+        for c in range(3):
+            row = ab[c + 1, pl.ds(y, 1), :]
+            for z0, n in spans:
+                lhs.append(tzb[pl.ds(z0, n), :] * row)
+        res = dot3(split(jnp.concatenate(lhs, axis=0)), (txb[0], txb[1]), ((1,), (1,)))
+        at = 0
+        for c in range(3):
+            for z0, n in spans:
+                sb[c, y, pl.ds(z0, n), :] = sb[c, y, pl.ds(z0, n), :] + res[at:at + n]
+                at += n
 
     @pl.when(is_src)
     def _():
@@ -471,84 +501,83 @@
         srcq = srcq + jnp.dot(e1, sel[1], precision=HI, preferred_element_type=F32)
         for c in range(3):
             ab[c + 1] = section_step * ab[0] * srcq[c:c + 1, :]
-
-    def move_x(y):
-        for c in range(3):
-            for z0 in range(0, CZ, CHUNK):
-                f = sb[c, y, pl.ds(z0, CHUNK), :]
-                g = wx[2, y, pl.ds(z0, CHUNK), :] * f
+        run(CY, lambda y: smear_rows(y, RIM))
+
+    def move_x(y, rows):
+        for z0, n in rows:
+            for c in range(3):
+                f = sb[c, y, pl.ds(z0, n), :]
+                g = wx[2, y, pl.ds(z0, n), :] * f
                 for k in (0, 1, 3, 4):
-                    p = wx[k, y, pl.ds(z0, CHUNK), :] * f
+                    p = wx[k, y, pl.ds(z0, n), :] * f
                     g = g + pltpu.roll(p, (k - 2) % NX, 1)
-                mb[c, y + 2, pl.ds(z0, CHUNK), :] = g
-
-    def smear_loop(y, carry):
-        for c in range(3):
-            lhs = split(tzq * ab[c + 1, pl.ds(y, 1), :])
-            sb[c, y] = sb[c, y] + dot3(lhs, txs, ((1,), (1,)))
-        return carry
+                mb[c, y + 2, pl.ds(z0, n), :] = g
+
+    def m_copy(d, part):
+        src_y, dst_y = (CY, 0) if d == 0 else (2, CY + 2)
+        z0, n = PARTS[part]
+        return rcopy(mb.at[:, pl.ds(src_y, 2), pl.ds(z0, n)], mb.at[:, pl.ds(dst_y, 2), pl.ds(z0, n)],
+                     ms.at[d, part], mr.at[d, part], (gy + (1 if d == 0 else -1), gz))
+
+    run(4, lambda i: move_x(edge_y(i), RIM))
+    for d in range(2):
+        @pl.when(up_cond[d][0])
+        def _():
+            for part in range(2):
+                m_copy(d, part).start()
+
+    @pl.when(in_span)
+    def _():
+        for d in range(1, n_zc):
+            p3_copy(d).start()
+
+    for f in range(2):
+        for d in range(2):
+            @pl.when(up_cond[d][1])
+            def _():
+                y_copy(f, d, 2).wait_recv()
+
+    run(4, lambda i: section_rows(edge_y(i), MID))
 
     @pl.when(is_src)
     def _():
-        lax.fori_loop(0, CY, smear_loop, 0)
-
-    def edge_loop(i, carry):
-        move_x(jnp.where(i < 2, i, i + CY - 4))
-        return carry
-
-    lax.fori_loop(0, 4, edge_loop, 0)
-
-    def m_copy(d):
-        src_y, dst_y = (CY, 0) if d == 0 else (2, CY + 2)
-        return rcopy(mb.at[:, pl.ds(src_y, 2)], mb.at[:, pl.ds(dst_y, 2)],
-                     ms.at[d], mr.at[d], (gy + (1 if d == 0 else -1), gz))
-
+        run(4, lambda i: smear_rows(edge_y(i), MID))
+
+    run(4, lambda i: move_x(edge_y(i), MID))
     for d in range(2):
         @pl.when(up_cond[d][0])
         def _():
-            m_copy(d).start()
-
-    def mid_loop(i, carry):
-        move_x(i + 2)
-        return carry
-
-    lax.fori_loop(0, CY - 4, mid_loop, 0)
-
-    def move_y(y):
-        for z0 in range(0, CZ, CHUNK):
-            w = [wy[k, y + 4 - k, pl.ds(z0, CHUNK), :] for k in range(5)]
+            m_copy(d, 2).start()
+
+    run(CY - 4, lambda i: move_x(i + 2, RIM))
+
+    def move_y(y, rows):
+        for z0, n in rows:
+            w = [wy[k, y + 4 - k, pl.ds(z0, n), :] for k in range(5)]
             for c in range(3):
-                g = w[0] * mb[c, y + 4, pl.ds(z0, CHUNK), :]
+                g = w[0] * mb[c, y + 4, pl.ds(z0, n), :]
                 for k in range(1, 5):
-                    g = g + w[k] * mb[c, y + 4 - k, pl.ds(z0, CHUNK), :]
-                yb[c, y, pl.ds(8 + z0, CHUNK), :] = g
-
-    def mid_y(i, carry):
-        move_y(i + 2)
-        return carry
-
-    lax.fori_loop(0, CY - 4, mid_y, 0)
+                    g = g + w[k] * mb[c, y + 4 - k, pl.ds(z0, n), :]
+                yb[c, y, pl.ds(8 + z0, n), :] = g
+
+    run(CY - 4, lambda i: move_y(i + 2, RIM))
     for d in range(2):
         @pl.when(up_cond[d][1])
         def _():
-            m_copy(d).wait_recv()
-
-    def edge_y(i, carry):
-        move_y(jnp.where(i < 2, i, i + CY - 4))
-        return carry
-
-    lax.fori_loop(0, 4, edge_y, 0)
-
-    def pack2(i, carry):
+            for part in range(2):
+                m_copy(d, part).wait_recv()
+
+    run(4, lambda i: move_y(edge_y(i), RIM))
+
+    def pack2(i):
         c = i // 4
         g = i % 4
         for j in range(4):
             y = 4 * g + j
             ks[0, c, g, 2 * j:2 * j + 2, :] = yb[c, y, 6 + CZ:8 + CZ, :]
             ks[1, c, g, 2 * j:2 * j + 2, :] = yb[c, y, 8:10, :]
-        return carry
-
-    lax.fori_loop(0, 12, pack2, 0)
+
+    run(12, pack2)
 
     def k_copy(d):
         return rcopy(ks.at[d], kr.at[d], kss.at[d], ksr.at[d], (gy, gz + (1 if d == 0 else -1)))
@@ -557,32 +586,32 @@
         @pl.when(rt_cond[d][0])
         def _():
             k_copy(d).start()
-    for d in range(2):
-        @pl.when(rt_cond[d][1])
-        def _():
-            k_copy(d).wait_recv()
-            lo = 6 if d == 0 else 8 + CZ
-
-            def unpack2(i, carry):
-                c = i // 4
-                g = i % 4
-                for j in range(4):
-                    yb[c, 4 * g + j, lo:lo + 2, :] = kr[d, c, g, 2 * j:2 * j + 2, :]
-                return carry
-
-            lax.fori_loop(0, 12, unpack2, 0)
-
-    def move_z(y, carry):
-        for z0 in range(0, CZ, CHUNK):
-            w = [wz[k, y, pl.ds(8 + z0 + 2 - k, CHUNK), :] for k in range(5)]
+
+    @pl.when(is_src)
+    def _():
+        run(CY - 4, lambda i: smear_rows(i + 2, MID))
+
+    run(CY - 4, lambda i: move_x(i + 2, MID))
+    for y in (0, 1, CY + 2, CY + 3):
+        wy_one(y, MID)
+    run(CY - 4, lambda i: move_y(i + 2, MID))
+    for d in range(2):
+        @pl.when(up_cond[d][1])
+        def _():
+            m_copy(d, 2).wait_recv()
+
+    run(4, lambda i: move_y(edge_y(i), MID))
+
+    def move_z(y, rows):
+        for z0, n in rows:
+            w = [wz[k, y, pl.ds(8 + z0 + 2 - k, n), :] for k in range(5)]
             for c in range(3):
-                g = w[0] * yb[c, y, pl.ds(8 + z0 + 2, CHUNK), :]
+                g = w[0] * yb[c, y, pl.ds(8 + z0 + 2, n), :]
                 for k in range(1, 5):
-                    g = g + w[k] * yb[c, y, pl.ds(8 + z0 + 2 - k, CHUNK), :]
-                out_ref[c, y, pl.ds(z0, CHUNK), :] = g
-        return carry
-
-    lax.fori_loop(0, CY, move_z, 0)
+                    g = g + w[k] * yb[c, y, pl.ds(8 + z0 + 2 - k, n), :]
+                out_ref[c, y, pl.ds(z0, n), :] = g
+
+    run(CY, lambda y: move_z(y, MID))
 
     for s in range(n_zc):
         @pl.when((zc != s) & (s * 8 + plane < NS))
@@ -614,6 +643,22 @@
             src_out[c:c + 1, 128 * r:128 * r + 128] = full[c][r:r + 1]
 
     for d in range(2):
+        @pl.when(rt_cond[d][1])
+        def _():
+            k_copy(d).wait_recv()
+            lo = 6 if d == 0 else 8 + CZ
+
+            def unpack2(i):
+                c = i // 4
+                g = i % 4
+                for j in range(4):
+                    yb[c, 4 * g + j, lo:lo + 2, :] = kr[d, c, g, 2 * j:2 * j + 2, :]
+
+            run(12, unpack2)
+
+    run(CY, lambda y: move_z(y, RIM))
+
+    for d in range(2):
         @pl.when(rt_cond[d][0])
         def _():
             z_copy(d).wait_send()
@@ -621,9 +666,10 @@
 
         @pl.when(up_cond[d][0])
         def _():
-            y_copy(0, d).wait_send()
-            y_copy(1, d).wait_send()
-            m_copy(d).wait_send()
+            for part in range(3):
+                y_copy(0, d, part).wait_send()
+                y_copy(1, d, part).wait_send()
+                m_copy(d, part).wait_send()
 
     @pl.when(is_src)
     def _():
@@ -672,9 +718,11 @@
         V((5, 16, 128), F32),
         V((TURBINES, 8, 128), F32),
         V((4, cy, 128), F32),
-        D((6,)), D((2, 2)), D((2, 2)), D((2,)), D((2,)),
+        V((2, nx, 128), BF),
+        V((cz, 128), F32),
+        D((6,)), D((2, 2, 3)), D((2, 2, 3)), D((2,)), D((2,)),
         D((n_z - 1,)), D((nvb,)), D((n_y // TURBINES - 1,)), D((n_y // TURBINES,)), D((n_zc - 1,)), D((n_zc,)),
-        D((2,)), D((2,)), D((2,)), D((2,)),
+        D((2, 3)), D((2, 3)), D((2,)), D((2,)),
     ]
     out, src = pl.pallas_call(
         functools.partial(kernel, n_y, n_z),

time: 54.3 us -> 47.9 us (0.88)
  the two profiles are of different devices: /device:TPU:262 before, /device:TPU:248 now
where the time goes in v3:
time: 47.9 us; the launch traced here: 47.7 us
  Pallas kernels  44.7 us (93%)
  local copies, waits for them, and re-layouts  1.76 us (4%)
  between operations  1.3 us (3%)
    pallas_call x1, Pallas kernels, on_device(): pl.pallas_call(functools.partial(kernel, n_y, n_z), name='section', out_s...  44.7 us
    unnamed x4, local copies, waits for them, and re-layouts  1.76 us

profile of v3, /device:TPU:248, one launch (start us, length us, event | category | flops | bytes accessed | tf_op | source)
XLA Modules:
  0.0 47.7 jit_solution(5841690282577521062)
XLA Ops:
  1.3 44.7 %section.1 = (f32[3,16,64,128]{3,2,1,0:T(8,128)S(1)}, f32[3,1152]{1,0:T(4,128)}) custom-call(f32[3,16,64,128]{3,2,1,0:T(8,128)} %om_hbm.1, f32[3,16,64,128]{3,2,1,0:T(8,128)} %ve_hbm.1, s32[1152]{0:T(1024)} %own_ref.1, s32[3,1152]{1,0:T(4,128)} %cell_ref.1, f32[3,1152]{1,0:T(4,128)} %frac_ref.1, f32[1152]{0:T(1024)} %chord_ref.1, f32[1152]{0:T(1024)} %twist_ref.1, ...), custom_call_target="tpu_custom_call" | custom-call | tf_op jit(solution)/shard_map/section/pallas_call | solution.py:727
  46.0 0.0 copy-start
  46.0 1.1 %copy.12 = f32[3,16,64,128]{3,2,1,0:T(8,128)} copy(f32[3,16,64,128]{3,2,1,0:T(8,128)S(1)} %get-tuple-element.2) | data formatting | bytes 3145728
  47.1 0.0 copy-done
  47.1 0.6 %copy.14 = f32[3,1152]{1,0:T(4,128)} copy(f32[3,1152]{1,0:T(4,128)S(1)} %copy-done) | data formatting | bytes 27648
Async XLA Ops:
  46.0 1.2 %copy-start = (f32[3,1152]{1,0:T(4,128)S(1)}, f32[3,1152]{1,0:T(4,128)}, u32[]{:S(2)}) copy-start(f32[3,1152]{1,0:T(4,128)} %get-tuple-element.7) | copy-start | bytes 41476

commit v4 on v3

--- a/solution.py
+++ b/solution.py
@@ -65,10 +65,10 @@
 
 def kernel(
     n_y, n_z,
-    om_hbm, ve_hbm, own_ref, cell_ref, frac_ref, chord_ref, twist_ref, ang_ref,
+    om_hbm, ve_hbm, own_h, cell_h, frac_h, chord_h, twist_h, ang_h,
     out_ref, src_out,
     vb, wb, sb, mb, yb, wx, wy, wz, zs, zr, ks, kr,
-    vals, sel, pk, p1r, p2s, p2r, p3s, p3r, pvb, tall, ab, txb, tzb,
+    vals, sel, pk, p1r, p2s, p2r, p3s, p3r, pvb, tall, ab, txb, tzb, own_ref, cell_ref, frac_ref, chord_ref, twist_ref, ang_ref,
     ld_sem, ys, yr, zss, zsr, p1s, p1v, p2ss, p2v, p3ss, p3v, ms, mr, kss, ksr,
 ):
     gy = lax.axis_index("gy")
@@ -121,6 +121,14 @@
         pl.semaphore_signal(bar, inc=1, device_id=(gy + 1, gz), device_id_type=MESH)
 
     loads = []
+    small = []
+    for i, (src, dst) in enumerate((
+        (own_h, own_ref), (cell_h, cell_ref), (frac_h, frac_ref),
+        (chord_h, chord_ref), (twist_h, twist_ref), (ang_h, ang_ref),
+    )):
+        small.append(pltpu.make_async_copy(src, dst, ld_sem.at[6 + i]))
+    for cp in small:
+        cp.start()
     for c in range(3):
         loads.append(pltpu.make_async_copy(
             ve_hbm.at[c], vb.at[c, pl.ds(2, CY), pl.ds(8, CZ)], ld_sem.at[c]))
@@ -158,6 +166,8 @@
     def _():
         zero_y(CY + 2)
 
+    for cp in small:
+        cp.wait()
     vals[0:3, :] = cell_ref[...].astype(F32)
     vals[3:6, :] = frac_ref[...]
     my_block = gy * n_z + gz
@@ -308,13 +318,12 @@
         def _():
             z_copy(d).start()
 
-    for parts in ((0, 1), (2,)):
-        for d in range(2):
-            @pl.when(up_cond[d][0])
-            def _():
-                for f in range(2):
-                    for part in parts:
-                        y_copy(f, d, part).start()
+    for d in range(2):
+        @pl.when(up_cond[d][0])
+        def _():
+            for f in range(2):
+                for part in range(2):
+                    y_copy(f, d, part).start()
 
     def wx_loop(y, carry):
         lanes = lax.broadcasted_iota(jnp.int32, (CHUNK, NX), 1)
@@ -371,23 +380,23 @@
             res.append(jnp.where(m, r, 0.0))
         return res
 
-    def section_rows(y, rows):
+    def section_rows(y, rows, dims=(0, 1, 2)):
         for z0, n in rows:
             om = [wb[c, y + 2, pl.ds(8 + z0, n), :] for c in range(3)]
-            oms = [c0 * o for o in om]
+            oms = {d: c0 * om[2 - d] for d in dims}
             for c in range(3):
-                acc = om[c]
+                acc = om[c] if 0 in dims else sb[c, y, pl.ds(z0, n), :]
                 near = None
                 far = None
-                for dim in range(3):
+                for dim in dims:
                     a = around(vb, c, y, z0, n, dim)
-                    acc = acc + oms[2 - dim] * (8.0 * (a[2] - a[1]) - (a[3] - a[0]))
+                    acc = acc + oms[dim] * (8.0 * (a[2] - a[1]) - (a[3] - a[0]))
                     b = around(wb, c, y, z0, n, dim)
                     p = b[1] + b[2]
                     e = b[0] + b[3]
                     near = p if near is None else near + p
                     far = e if far is None else far + e
-                acc = acc + cl * (16.0 * near - far - 90.0 * om[c])
+                acc = acc + cl * (16.0 * near - far - (30.0 * len(dims)) * om[c])
                 sb[c, y, pl.ds(z0, n), :] = acc
 
     RIM = ((0, 8), (CZ - 8, 8))
@@ -406,6 +415,7 @@
 
     lax.fori_loop(0, CY, wx_loop, 0)
     run(CY - 4, lambda i: section_rows(i + 2, MID))
+    run(4, lambda i: section_rows(edge_y(i), MID, (0, 1)))
 
     def p1_wait(s):
         return rcopy(p1r.at[s], p1r.at[s], p1s.at[0], p1v.at[s], (gy, gz))
@@ -427,6 +437,12 @@
         for d in range(1, span):
             p2_copy(d).start()
 
+    for d in range(2):
+        @pl.when(up_cond[d][0])
+        def _():
+            y_copy(0, d, 2).start()
+            y_copy(1, d, 2).start()
+
     lax.fori_loop(0, CY, wz_loop, 0)
     lax.fori_loop(0, CY, wy_loop, 0)
 
@@ -447,6 +463,7 @@
             lax.fori_loop(0, 12, unpack, 0)
 
     lax.fori_loop(0, CY, wz_edge, 0)
+    run(4, lambda i: section_rows(edge_y(i), RIM, (0, 1)))
     run(CY - 4, lambda i: section_rows(i + 2, RIM))
 
     for f in range(2):
@@ -456,7 +473,7 @@
                 for part in range(2):
                     y_copy(f, d, part).wait_recv()
 
-    run(4, lambda i: section_rows(edge_y(i), RIM))
+    run(4, lambda i: section_rows(edge_y(i), RIM, (2,)))
     for y in (0, 1, CY + 2, CY + 3):
         wy_one(y, RIM)
 
@@ -501,7 +518,7 @@
         srcq = srcq + jnp.dot(e1, sel[1], precision=HI, preferred_element_type=F32)
         for c in range(3):
             ab[c + 1] = section_step * ab[0] * srcq[c:c + 1, :]
-        run(CY, lambda y: smear_rows(y, RIM))
+        run(4, lambda i: smear_rows(edge_y(i), RIM))
 
     def move_x(y, rows):
         for z0, n in rows:
@@ -531,13 +548,17 @@
         for d in range(1, n_zc):
             p3_copy(d).start()
 
+    @pl.when(is_src)
+    def _():
+        run(CY - 4, lambda i: smear_rows(i + 2, RIM))
+
     for f in range(2):
         for d in range(2):
             @pl.when(up_cond[d][1])
             def _():
                 y_copy(f, d, 2).wait_recv()
 
-    run(4, lambda i: section_rows(edge_y(i), MID))
+    run(4, lambda i: section_rows(edge_y(i), MID, (2,)))
 
     @pl.when(is_src)
     def _():
@@ -690,7 +711,6 @@
     n_zc = n_y // 8
     vm = pl.BlockSpec(memory_space=pltpu.VMEM)
     hb = pl.BlockSpec(memory_space=pl.ANY)
-    sm = pl.BlockSpec(memory_space=pltpu.SMEM)
     nvb = max(n_z // 2, 1)
     V = pltpu.VMEM
     D = pltpu.SemaphoreType.DMA
@@ -720,7 +740,9 @@
         V((4, cy, 128), F32),
         V((2, nx, 128), BF),
         V((cz, 128), F32),
-        D((6,)), D((2, 2, 3)), D((2, 2, 3)), D((2,)), D((2,)),
+        V((n_p,), jnp.int32), V((3, n_p), jnp.int32), V((3, n_p), F32), V((n_p,), F32), V((n_p,), F32),
+        pltpu.SMEM((1,), jnp.int32),
+        D((12,)), D((2, 2, 3)), D((2, 2, 3)), D((2,)), D((2,)),
         D((n_z - 1,)), D((nvb,)), D((n_y // TURBINES - 1,)), D((n_y // TURBINES,)), D((n_zc - 1,)), D((n_zc,)),
         D((2, 3)), D((2, 3)), D((2,)), D((2,)),
     ]
@@ -729,9 +751,9 @@
         name="section",
         out_shape=(
             pltpu.VMEM(omega.shape, F32),
-            jax.ShapeDtypeStruct((3, n_p), F32),
+            V((3, n_p), F32),
         ),
-        in_specs=[hb, hb, vm, vm, vm, vm, vm, sm],
+        in_specs=[hb] * 8,
         out_specs=(vm, vm),
         scratch_shapes=scratch,
         compiler_params=pltpu.CompilerParams(

time: 47.9 us -> 43.5 us (0.908)
  the two profiles are of different devices: /device:TPU:248 before, /device:TPU:40 now
where the time goes in v4:
time: 43.5 us; the launch traced here: 43.4 us
  Pallas kernels  40.3 us (93%)
  local copies, waits for them, and re-layouts  1.75 us (4%)
  between operations  1.29 us (3%)
    pallas_call x1, Pallas kernels, on_device(): pl.pallas_call(functools.partial(kernel, n_y, n_z), name='section', out_s...  40.3 us
    unnamed x2, local copies, waits for them, and re-layouts  1.75 us

profile of v4, /device:TPU:40, one launch (start us, length us, event | category | flops | bytes accessed | tf_op | source)
XLA Modules:
  0.0 43.4 jit_solution(8502270008250651505)
XLA Ops:
  1.3 40.3 %section.1 = (f32[3,16,64,128]{3,2,1,0:T(8,128)S(1)}, f32[3,1152]{1,0:T(4,128)S(1)}) custom-call(f32[3,16,64,128]{3,2,1,0:T(8,128)} %om_hbm.1, f32[3,16,64,128]{3,2,1,0:T(8,128)} %ve_hbm.1, s32[1152]{0:T(1024)} %own_h.1, s32[3,1152]{1,0:T(4,128)} %cell_h.1, f32[3,1152]{1,0:T(4,128)} %frac_h.1, f32[1152]{0:T(1024)} %chord_h.1, f32[1152]{0:T(1024)} %twist_h.1, ...), custom_call_target="tpu_custom_call" | custom-call | tf_op jit(solution)/shard_map/section/pallas_call | solution.py:749
  41.6 1.1 %copy.12 = f32[3,16,64,128]{3,2,1,0:T(8,128)} copy(f32[3,16,64,128]{3,2,1,0:T(8,128)S(1)} %get-tuple-element.2) | data formatting | bytes 3145728
  42.8 0.6 %copy.13 = f32[3,1152]{1,0:T(4,128)} copy(f32[3,1152]{1,0:T(4,128)S(1)} %get-tuple-element.3) | data formatting | bytes 27648

commit v5 on v4

--- a/solution.py
+++ b/solution.py
@@ -491,18 +491,20 @@
         p3s[...] = tile
         p3r[zc] = tile
 
-    def smear_rows(y, spans):
+    def smear_rows(ys, spans):
         lhs = []
-        for c in range(3):
-            row = ab[c + 1, pl.ds(y, 1), :]
-            for z0, n in spans:
-                lhs.append(tzb[pl.ds(z0, n), :] * row)
+        for y in ys:
+            for c in range(3):
+                row = ab[c + 1, pl.ds(y, 1), :]
+                for z0, n in spans:
+                    lhs.append(tzb[pl.ds(z0, n), :] * row)
         res = dot3(split(jnp.concatenate(lhs, axis=0)), (txb[0], txb[1]), ((1,), (1,)))
         at = 0
-        for c in range(3):
-            for z0, n in spans:
-                sb[c, y, pl.ds(z0, n), :] = sb[c, y, pl.ds(z0, n), :] + res[at:at + n]
-                at += n
+        for y in ys:
+            for c in range(3):
+                for z0, n in spans:
+                    sb[c, y, pl.ds(z0, n), :] = sb[c, y, pl.ds(z0, n), :] + res[at:at + n]
+                    at += n
 
     @pl.when(is_src)
     def _():
@@ -518,7 +520,7 @@
         srcq = srcq + jnp.dot(e1, sel[1], precision=HI, preferred_element_type=F32)
         for c in range(3):
             ab[c + 1] = section_step * ab[0] * srcq[c:c + 1, :]
-        run(4, lambda i: smear_rows(edge_y(i), RIM))
+        smear_rows((0, 1, CY - 2, CY - 1), RIM)
 
     def move_x(y, rows):
         for z0, n in rows:
@@ -536,8 +538,9 @@
         return rcopy(mb.at[:, pl.ds(src_y, 2), pl.ds(z0, n)], mb.at[:, pl.ds(dst_y, 2), pl.ds(z0, n)],
                      ms.at[d, part], mr.at[d, part], (gy + (1 if d == 0 else -1), gz))
 
-    run(4, lambda i: move_x(edge_y(i), RIM))
-    for d in range(2):
+    for d in range(2):
+        run(2, lambda i: move_x(i + (CY - 2 if d == 0 else 0), RIM))
+
         @pl.when(up_cond[d][0])
         def _():
             for part in range(2):
@@ -550,7 +553,7 @@
 
     @pl.when(is_src)
     def _():
-        run(CY - 4, lambda i: smear_rows(i + 2, RIM))
+        run((CY - 4) // 4, lambda i: smear_rows([4 * i + 2 + j for j in range(4)], RIM))
 
     for f in range(2):
         for d in range(2):
@@ -558,14 +561,16 @@
             def _():
                 y_copy(f, d, 2).wait_recv()
 
-    run(4, lambda i: section_rows(edge_y(i), MID, (2,)))
-
-    @pl.when(is_src)
-    def _():
-        run(4, lambda i: smear_rows(edge_y(i), MID))
-
-    run(4, lambda i: move_x(edge_y(i), MID))
-    for d in range(2):
+    for d in range(2):
+        off = CY - 2 if d == 0 else 0
+        run(2, lambda i: section_rows(i + off, MID, (2,)))
+
+        @pl.when(is_src)
+        def _():
+            smear_rows((off, off + 1), MID)
+
+        run(2, lambda i: move_x(i + off, MID))
+
         @pl.when(up_cond[d][0])
         def _():
             m_copy(d, 2).start()
@@ -610,7 +615,7 @@
 
     @pl.when(is_src)
     def _():
-        run(CY - 4, lambda i: smear_rows(i + 2, MID))
+        run((CY - 4) // 2, lambda i: smear_rows((2 * i + 2, 2 * i + 3), MID))
 
     run(CY - 4, lambda i: move_x(i + 2, MID))
     for y in (0, 1, CY + 2, CY + 3):

time: 43.5 us -> 41.4 us (0.952)
  Pallas kernels: 40.3 us -> 38.2 us
    pallas_call x1, Pallas kernels: 40.3 us -> 38.2 us  [on_device(): pl.pallas_call(functools.partial(kernel, n_y, n_z), name='section', out_s...]
where the time goes in v5:
time: 41.4 us; the launch traced here: 41.2 us
  Pallas kernels  38.2 us (92%)
  local copies, waits for them, and re-layouts  1.75 us (4%)
  between operations  1.29 us (3%)
    pallas_call x1, Pallas kernels, on_device(): pl.pallas_call(functools.partial(kernel, n_y, n_z), name='section', out_s...  38.2 us
    unnamed x2, local copies, waits for them, and re-layouts  1.75 us

profile of v5, /device:TPU:40, one launch (start us, length us, event | category | flops | bytes accessed | tf_op | source)
XLA Modules:
  0.0 41.2 jit_solution(17907447386677064572)
XLA Ops:
  1.3 38.2 %section.1 = (f32[3,16,64,128]{3,2,1,0:T(8,128)S(1)}, f32[3,1152]{1,0:T(4,128)S(1)}) custom-call(f32[3,16,64,128]{3,2,1,0:T(8,128)} %om_hbm.1, f32[3,16,64,128]{3,2,1,0:T(8,128)} %ve_hbm.1, s32[1152]{0:T(1024)} %own_h.1, s32[3,1152]{1,0:T(4,128)} %cell_h.1, f32[3,1152]{1,0:T(4,128)} %frac_h.1, f32[1152]{0:T(1024)} %chord_h.1, f32[1152]{0:T(1024)} %twist_h.1, ...), custom_call_target="tpu_custom_call" | custom-call | tf_op jit(solution)/shard_map/section/pallas_call | solution.py:754
  39.5 1.1 %copy.12 = f32[3,16,64,128]{3,2,1,0:T(8,128)} copy(f32[3,16,64,128]{3,2,1,0:T(8,128)S(1)} %get-tuple-element.2) | data formatting | bytes 3145728
  40.6 0.6 %copy.13 = f32[3,1152]{1,0:T(4,128)} copy(f32[3,1152]{1,0:T(4,128)S(1)} %get-tuple-element.3) | data formatting | bytes 27648
